TPU v7x, 256 devices: a whole 4x4x8 slice. The times are simulated.
256 devices in a mesh: gx: 8 (over y, x_lo), gy: 4 (over x_hi, core), gz: 8 (over z).
Axes of the slice: x: 4 (x_hi: 2, x_lo: 2; x = x_hi * 2 + x_lo), y: 4, z: 8, core: 2. Of those that a mesh axis runs over, the one named last changes fastest.
Arguments:
- occupancy: int32 [128, 256, 1024], P('gx', 'gy', 'gz'), may hold values 0 or 1
- site_field: float32 [128, 256, 1024], P('gx', 'gy', 'gz'), may hold values from -6 to 6
- attempt_rate: float32 [128, 256, 1024], P('gx', 'gy', 'gz'), may hold values from 0.2 to 5
- uniforms: float32 [8, 128, 256, 512], P(None, 'gx', 'gy', 'gz'), may hold values from 0.001 to 1
Outputs:
- final_spins: float32 [128, 256, 1024], P('gx', 'gy', 'gz')
- history: float32 [2, 8], replicated
All inputs are finite; a program needn't handle non-finite values. No bound on the sum of `occupancy` on one device may be relied on, other than what follows from the above.
Results may differ from a plain program's by a relative error of at most 0.0002.
Values sent between devices are 32-bit elements; how exact they have to be, the bound alone decides.
No kernel may reach another device: no remote copies, remote signals or barrier semaphores. Data moves between devices by JAX's collectives and lax.ppermute only.
A program may use at most 128 MiB of HBM per device.

v0:
```python
import functools

import jax
import jax.numpy as jnp
from jax import lax
from jax.experimental import pallas as pl
from jax.experimental.pallas import tpu as pltpu
from jax.sharding import PartitionSpec as P


SECTIONS = 8
AXES = ("gx", "gy", "gz")
BX, BY, BZ = 16, 64, 128
HY, HZ = BY // 2, BZ // 2
UNROLL = 4
CHUNK = 4
PITCH = HY + 8
F32, BF16 = jnp.float32, jnp.bfloat16


def lane_of(rows=HY):
    return lax.broadcasted_iota(jnp.int32, (rows, BZ), 1)


def odd_row(shift, rows=HY):
    return (lax.broadcasted_iota(jnp.int32, (rows, BZ), 0) + shift) % 2 == 1


def roll(value, shift):
    shift = shift % BZ
    return value if shift == 0 else pltpu.roll(value, shift, 1)


def shuffle_matrix(transposed):
    major = lax.broadcasted_iota(jnp.int32, (BZ, BZ), 1 if transposed else 0)
    minor = lax.broadcasted_iota(jnp.int32, (BZ, BZ), 0 if transposed else 1)
    return (minor == major // 2 + HZ * (major % 2)).astype(F32)


def matmul(a, b, exact):
    precision = lax.Precision.HIGHEST if exact else lax.Precision.DEFAULT
    return jnp.dot(a, b, precision=precision, preferred_element_type=F32)


def face_column(plane, x, phase):
    ends = jnp.where(odd_row(x + phase), roll(plane, HZ + 1), plane)
    return roll(ends, x)


def fetch(pairs, arrived):
    copies = [pltpu.make_async_copy(source, target, arrived.at[i]) for i, (source, target) in enumerate(pairs)]
    for copy in copies:
        copy.start()
    return copies


def split_sites(mixed, odd, low):
    lower, upper = mixed[:HY], mixed[HY:]
    lower_turned, upper_turned = roll(lower, HZ), roll(upper, HZ)
    even_site = jnp.where(low, jnp.where(odd, lower_turned, lower), jnp.where(odd, upper, upper_turned))
    odd_site = jnp.where(low, jnp.where(odd, lower, lower_turned), jnp.where(odd, upper_turned, upper))
    return even_site, odd_site


def spins_kernel(occ_hbm, spin, xlo, xhi, ylo, yhi, zed, occ, arrived):
    copies = fetch([(occ_hbm.at[pl.ds(c * CHUNK, CHUNK)], occ.at[pl.ds(c * CHUNK, CHUNK)]) for c in range(BX // CHUNK)], arrived)
    lane = lane_of()
    wide = shuffle_matrix(False)
    columns = [jnp.zeros((HY, BZ), F32)] * 2
    for x in range(BX):
        if x % CHUNK == 0:
            copies[x // CHUNK].wait()
        planes = split_sites(matmul(2.0 * occ[x].astype(F32) - 1.0, wide, False), odd_row(x), lane < HZ)
        for p, plane in enumerate(planes):
            spin[p, x + 1, :HY] = plane
            ylo[p, x : x + 1] = plane[:1]
            yhi[p, x : x + 1] = plane[HY - 1 :]
            columns[p] = jnp.where(lane % HZ == x, face_column(plane, x, p), columns[p])
            if x == 0:
                xlo[p] = plane
            if x == BX - 1:
                xhi[p] = plane
    for p in range(2):
        zed[p] = columns[p]


def shuffled(value, wide):
    high = value.astype(BF16)
    rest = value - high.astype(F32)
    middle = rest.astype(BF16)
    low = (rest - middle.astype(F32)).astype(BF16)
    rows = value.shape[0]
    parts = jnp.dot(jnp.concatenate([high, middle, low], axis=0), wide, preferred_element_type=F32)
    return parts[:rows] + parts[rows : 2 * rows] + parts[2 * rows :]


def fields_kernel(
    field_hbm, attempt_hbm, uniforms, h, a, v0, v_out, field, attempt, raw, inverse, v, arrived, drawn, left,
):
    copies = fetch([(field_hbm, field), (attempt_hbm, attempt)], arrived)
    draws = fetch([(uniforms.at[k], raw.at[k]) for k in range(SECTIONS)], drawn)
    low = lane_of() < HZ
    wide = shuffle_matrix(False).astype(BF16)
    for copy in copies:
        copy.wait()

    @pl.loop(0, BX // UNROLL)
    def _(i):
        for j in range(UNROLL):
            x = i * UNROLL + j
            h[0, x], h[1, x] = split_sites(shuffled(field[x], wide), odd_row(j), low)
            even_site, odd_site = split_sites(shuffled(attempt[x], wide), odd_row(j), low)
            a[0, x], a[1, x] = even_site, odd_site
            inverse[0, x], inverse[1, x] = 1.0 / even_site, 1.0 / odd_site

    writes = []
    for k in range(SECTIONS):
        draws[k].wait()

        @pl.loop(0, BX // UNROLL)
        def _(i):
            for j in range(UNROLL):
                x = i * UNROLL + j
                scaled = jnp.concatenate([raw[k, x, :HY], raw[k, x, HY:]], axis=1) * inverse[k % 2, x]
                if k == 0:
                    v0[x] = scaled
                else:
                    v[k, x] = scaled

        if k > 0:
            write = pltpu.make_async_copy(v.at[k], v_out.at[k], left.at[k])
            write.start()
            writes.append(write)
    for write in writes:
        write.wait()


def z_parts(phase):
    lane = lane_of()
    row = lax.broadcasted_iota(jnp.int32, (HY, BZ), 0)
    return (lane % HZ + row + phase) % 2 == 1


def flip_of(total, half):
    ratio = total / half
    square = ratio * ratio
    return lambda odds: 1.0 - 2.0 / (1.0 + odds * square)


def eighth(value):
    return value[0:8] + value[8:16] + value[16:24] + value[24:32]


def advance(k, p, half, gathered, halo, spin, side, column, odds, gain, h, energy, fields, clock):
    total = jnp.sum(jnp.sum(gathered[...], axis=0, keepdims=True), axis=1, keepdims=True)
    flip = flip_of(total, half)
    elapsed = clock[1:2, :] + half / total
    clock[1:2, :] = elapsed
    clock[0:1, :] = jnp.where(lane_of(1) == k - 1, elapsed, clock[0:1, :])
    of_gain = jnp.zeros((HY, BZ), F32)
    of_field = jnp.zeros((HY, BZ), F32)

    def step(i, carry):
        of_gain, of_field = carry
        for j in range(UNROLL):
            x = i * UNROLL + j
            new = spin[p, x + 1, :HY] * flip(odds[x])
            spin[p, x + 1, :HY] = new
            of_gain = of_gain + new * gain[x]
            of_field = of_field + new * h[p, x]
        return of_gain, of_field

    of_gain, of_field = lax.fori_loop(0, BX // UNROLL, step, (of_gain, of_field))
    fields[p] = eighth(of_field)
    energy[k - 1] = -eighth(of_gain) - fields[1 - p]
    if halo is None:
        return
    from_xlo, from_xhi, from_ylo, from_yhi, from_zlo, from_zhi = halo
    spin[p, 0, :HY] = spin[p, 0, :HY] * flip(from_xlo[...])
    spin[p, BX + 1, :HY] = spin[p, BX + 1, :HY] * flip(from_xhi[...])
    side[p] = side[p] * flip(jnp.where(lane_of(BX) < HZ, from_yhi[...], from_ylo[...]))
    column[p] = column[p] * flip(jnp.where(z_parts(p), from_zlo[...], from_zhi[...]))


def rates(act, spin, side, column, odds, gain, h, a, v, xlo, xhi, ylo, yhi, zed, sent):
    p = 1 - act
    lane = lane_of()
    one_row = lane_of(1)
    for x in range(BX):
        first, last = spin[p, x + 1, :1], spin[p, x + 1, HY - 1 : HY]
        beyond = side[p, x : x + 1]
        spin[p, x + 1, HY + 1 : HY + 2] = roll(jnp.where(one_row < HZ, last, beyond), HZ)
        spin[p, x + 1, HY : HY + 1] = roll(jnp.where(one_row < HZ, beyond, first), HZ)
    ends = column[p]
    top = lax.broadcasted_iota(jnp.int32, (HY, BZ), 0) == 0

    def step(i, carry):
        packed, summed = carry
        for j in range(UNROLL):
            x = i * UNROLL + j
            odd = odd_row(j + act)
            here = spin[p, x + 1, :HY]
            turned = jnp.where(odd, roll(here, -1), roll(here, 1))
            edge = jnp.where(odd, pltpu.roll(ends, (HZ - 1 - x) % BZ, 1), pltpu.roll(ends, (BZ - x) % BZ, 1))
            at_edge = lane % HZ == jnp.where(odd, HZ - 1, 0)
            beside = spin[p, x, :HY] + spin[p, x + 2, :HY]
            beside = beside + jnp.where(top, spin[p, x + 1, HY + 1 : HY + 2], pltpu.roll(here, 1, 0)) + spin[p, x + 1, 1 : HY + 1]
            beside = beside + here + jnp.where(at_edge, edge, turned)
            g = h[act, x] - 0.5 * beside
            gain[x] = g
            grown = 1.0 + jnp.exp(2.0 * spin[act, x + 1, :HY] * g)
            summed = summed + a[act, x] / grown
            root = v[x] * grown
            square = root * root
            odds[x] = square
            marked = jnp.where(odd, roll(square, HZ + 1), square)
            packed = jnp.where(lane % HZ == x, pltpu.roll(marked, x, 1), packed)
        return packed, summed

    packed, summed = lax.fori_loop(0, BX // UNROLL, step, (jnp.zeros((HY, BZ), F32), jnp.zeros((HY, BZ), F32)))
    xlo[...] = odds[0]
    xhi[...] = odds[BX - 1]
    for x in range(BX):
        ylo[x : x + 1] = odds[x, :1]
        yhi[x : x + 1] = odds[x, HY - 1 :]
    zed[...] = packed
    sent[...] = jnp.broadcast_to(jnp.sum(summed, axis=0, keepdims=True), sent.shape)


def first_kernel(
    from_xlo, from_xhi, from_ylo, from_yhi, from_zlo, from_zhi, h, a, v, v_hbm, spin_in,
    spin, side, column, energy, fields, clock, odds, gain, xlo, xhi, ylo, yhi, zed, sent, v_next, arrived,
):
    copies = fetch([(v_hbm.at[1], v_next)], arrived)
    for p in range(2):
        spin[p, 0, :HY] = from_xlo[p]
        spin[p, BX + 1, :HY] = from_xhi[p]
        side[p] = jnp.where(lane_of(BX) < HZ, from_yhi[p], from_ylo[p])
        column[p] = jnp.where(z_parts(p), from_zlo[p], from_zhi[p])
    of_field = jnp.zeros((HY, BZ), F32)
    for x in range(BX):
        of_field = of_field + spin[1, x + 1, :HY] * h[1, x]
    fields[0] = jnp.zeros((8, BZ), F32)
    fields[1] = eighth(of_field)
    energy[...] = jnp.zeros(energy.shape, F32)
    clock[...] = jnp.zeros(clock.shape, F32)
    rates(0, spin, side, column, odds, gain, h, a, v, xlo, xhi, ylo, yhi, zed, sent)
    copies[0].wait()


def section_kernel(
    act, half, where, gathered, from_xlo, from_xhi, from_ylo, from_yhi, from_zlo, from_zhi, h, a, v, v_hbm,
    spin_in, side_in, column_in, energy_in, fields_in, clock_in, odds_in, gain_in,
    spin, side, column, energy, fields, clock, odds, gain, xlo, xhi, ylo, yhi, zed, sent, v_next, arrived,
):
    k = where[0]
    copies = fetch([(v_hbm.at[jnp.minimum(k + 1, SECTIONS - 1)], v_next)], arrived)
    halo = (from_xlo, from_xhi, from_ylo, from_yhi, from_zlo, from_zhi)
    advance(k, 1 - act, half, gathered, halo, spin, side, column, odds, gain, h, energy, fields, clock)
    rates(act, spin, side, column, odds, gain, h, a, v, xlo, xhi, ylo, yhi, zed, sent)
    copies[0].wait()


def last_kernel(
    half, gathered, h, odds, gain, spin_in, energy_in, fields_in, clock_in,
    spin, energy, fields, clock, sent,
):
    advance(SECTIONS, (SECTIONS - 1) % 2, half, gathered, None, spin, None, None, odds, gain, h, energy, fields, clock)
    row = jnp.zeros((1, BZ), F32)
    for k in range(SECTIONS):
        value = jnp.sum(jnp.sum(energy[k], axis=0, keepdims=True), axis=1, keepdims=True)
        row = jnp.where(lane_of(1) == k, value, row)
    sent[...] = jnp.broadcast_to(row, sent.shape)


def unpack_kernel(spin, out):
    low = lane_of() < HZ
    narrow = shuffle_matrix(True)
    for x in range(BX):
        even_site, odd_site = spin[0, x + 1, :HY], spin[1, x + 1, :HY]
        odd = odd_row(x)
        even_z, odd_z = jnp.where(odd, odd_site, even_site), jnp.where(odd, even_site, odd_site)
        lower = jnp.where(low, even_z, roll(odd_z, HZ))
        upper = jnp.where(low, roll(even_z, HZ), odd_z)
        out[x, :HY] = matmul(lower, narrow, True)
        out[x, HY:] = matmul(upper, narrow, True)


def history_kernel(sites, gathered, clock, out):
    row = jnp.sum(gathered[...], axis=0, keepdims=True) / sites
    out[0:1, :] = row[:, :SECTIONS]
    out[1:2, :] = clock[0:1, :SECTIONS]


def call(kernel, inputs, outputs, aliases=None, far=(), far_out=(), scratch=(), flops=1000000):
    held, away = pl.BlockSpec(memory_space=pltpu.VMEM), pl.BlockSpec(memory_space=pltpu.HBM)
    inputs = [pltpu.with_memory_space_constraint(x, pltpu.HBM) if i in far else x for i, x in enumerate(inputs)]
    scalar = pl.BlockSpec(memory_space=pltpu.SMEM)
    return pl.pallas_call(
        kernel,
        out_shape=[pltpu.HBM(shape, F32) if i in far_out else jax.ShapeDtypeStruct(shape, F32) for i, shape in enumerate(outputs)],
        in_specs=[away if i in far else scalar if x.shape == (1,) else held for i, x in enumerate(inputs)],
        out_specs=[away if i in far_out else held for i in range(len(outputs))],
        input_output_aliases=aliases or {},
        scratch_shapes=scratch,
        compiler_params=pltpu.CompilerParams(vmem_limit_bytes=24 * 1024 * 1024),
        cost_estimate=pl.CostEstimate(flops=flops, bytes_accessed=1000000, transcendentals=0),
    )(*inputs)


def swap(xlo, xhi, ylo, yhi, zlo, zhi):
    got = []
    for axis, low, high in (("gx", xlo, xhi), ("gy", ylo, yhi), ("gz", zlo, zhi)):
        count = lax.axis_size(axis)
        up = [(i, (i + 1) % count) for i in range(count)]
        got.append(lax.ppermute(high, axis, up))
        got.append(lax.ppermute(low, axis, [(b, a) for a, b in up]))
    return got


def spread(sent):
    return lax.all_to_all(sent, AXES, 0, 0, tiled=True)


def body(occupancy, site_field, attempt_rate, uniforms):
    devices = lax.axis_size(AXES)
    sites = float(BX * BY * BZ * devices)
    half = sites / 2.0
    tile = (HY, BZ)
    spin_shape = (2, BX + 2, PITCH, BZ)
    block = (BX, *tile)
    faces = [tile, tile, (BX, BZ), (BX, BZ), tile]
    state = [spin_shape, (2, BX, BZ), (2, *tile), (SECTIONS, 8, BZ), (2, 8, BZ), (8, BZ), block, block]
    sent_shape = (devices, BZ)
    dma = pltpu.SemaphoreType.DMA
    streams = [dma((1,))]
    spin, *sides = call(
        spins_kernel, (occupancy,), [spin_shape] + [(2, *face) for face in faces], far=(0,),
        scratch=[pltpu.VMEM((BX, BY, BZ), jnp.int32), dma((BX // CHUNK,))],
    )
    halo = swap(*sides, sides[-1])
    h, a, v, draws = call(
        fields_kernel, (site_field, attempt_rate, uniforms), [(2, *block), (2, *block), block, (SECTIONS, *block)],
        far=(0, 1, 2), far_out=(3,),
        scratch=[
            pltpu.VMEM((BX, BY, BZ), F32), pltpu.VMEM((BX, BY, BZ), F32), pltpu.VMEM((SECTIONS, BX, BY, HZ), F32),
            pltpu.VMEM((2, *block), F32), pltpu.VMEM((SECTIONS, *block), F32),
            dma((2,)), dma((SECTIONS,)), dma((SECTIONS,)),
        ],
    )
    carried = call(
        first_kernel, (*halo, h, a, v, draws, spin), state + faces + [sent_shape, block], {10: 0}, far=(9,), scratch=streams,
    )

    def section(k, act, carried):
        *kept, xlo, xhi, ylo, yhi, zed, sent, v = carried
        gathered = spread(sent)
        halo = swap(xlo, xhi, ylo, yhi, zed, zed)
        return call(
            functools.partial(section_kernel, act, half),
            (jnp.full((1,), k, jnp.int32), gathered, *halo, h, a, v, draws, *kept), state + faces + [sent_shape, block],
            {12 + i: i for i in range(len(state))}, far=(11,), scratch=streams,
        )

    def pair(i, carried):
        return section(2 * i + 2, 0, section(2 * i + 1, 1, carried))

    carried = lax.fori_loop(0, SECTIONS // 2 - 1, pair, carried)
    carried = section(SECTIONS - 1, 1, carried)
    spin, _, _, energy, fields, clock, odds, gain = carried[: len(state)]
    gathered = spread(carried[-2])
    spin, energy, fields, clock, sent = call(
        functools.partial(last_kernel, half),
        (gathered, h, odds, gain, spin, energy, fields, clock),
        [spin_shape, state[3], state[4], state[5], sent_shape], {4: 0, 5: 1, 6: 2, 7: 3},
    )
    gathered = spread(sent)
    (final,) = call(unpack_kernel, (spin,), [(BX, BY, BZ)])
    (history,) = call(functools.partial(history_kernel, sites), (gathered, clock), [(2, SECTIONS)])
    return final, history


def solution(mesh):
    return jax.shard_map(
        body,
        mesh=mesh,
        in_specs=(P(*AXES), P(*AXES), P(*AXES), P(None, *AXES)),
        out_specs=(P(*AXES), P()),
        check_vma=False,
    )
```

profile of v0, /device:TPU:32, one launch (start us, length us, event | category | flops | bytes accessed | tf_op | source)
XLA Modules:
  0.0 248.2 jit_solution(7087490424279743215)
XLA Ops:
  0.6 2.5 shard_map.59
  3.2 1.6 collective-permute-start.12
  4.8 2.6 %collective-permute-start.13 = (f32[2,32,128]{2,1,0:T(8,128)S(1)}, f32[2,32,128]{2,1,0:T(8,128)S(1)}, u32[]{:S(2)}, u32[]{:S(2)}) collective-permute-start(f32[2,32,128]{2,1,0:T(8,128)S(1)} %get-tuple-element.383), channel_id=1, source_target_pairs={{32,0},{64,32},{96,64},{128,96},{160,128},{192,160},{224,192},{0,2... | collective-permute-start | bytes 98312 | tf_op jit(solution)/shard_map/ppermute | solution.py:317
  7.4 1.8 collective-permute-start.17
  9.4 2.9 %collective-permute-start.15 = (f32[2,16,128]{2,1,0:T(8,128)S(1)}, f32[2,16,128]{2,1,0:T(8,128)S(1)}, u32[]{:S(2)}, u32[]{:S(2)}) collective-permute-start(f32[2,16,128]{2,1,0:T(8,128)S(1)} %get-tuple-element.385), channel_id=1, source_target_pairs={{8,0},{16,8},{24,16},{0,24},{9,1},{17,9},{25,17},{1,25},{10,2},{18... | collective-permute-start | bytes 49160 | tf_op jit(solution)/shard_map/ppermute | solution.py:317
  12.4 7.3 %shard_map.60 = (f32[2,16,32,128]{3,2,1,0:T(8,128)S(1)}, f32[2,16,32,128]{3,2,1,0:T(8,128)S(1)}, f32[16,32,128]{2,1,0:T(8,128)S(1)}, f32[8,16,32,128]{3,2,1,0:T(8,128)}) custom-call(f32[16,64,128]{2,1,0:T(8,128)} %field_hbm.1, f32[16,64,128]{2,1,0:T(8,128)} %attempt_hbm.1, f32[8,16,64,64]{3,2,1,0:T(8,128)} %uniforms.1), custom_call_target="tpu_custom_call" | custom-call | flops 1000000 | bytes 1000000 | tf_op jit(solution)/shard_map/pallas_call | solution.py:299
  19.7 2.0 shard_map.61
  21.7 155.0 %while.41 = (s32[]{:T(128)}, f32[2,18,40,128]{3,2,1,0:T(8,128)S(1)}, f32[2,16,128]{2,1,0:T(8,128)S(1)}, f32[2,32,128]{2,1,0:T(8,128)S(1)}, f32[8,8,128]{2,1,0:T(...) while((s32[]{:T(128)}, ...), condition=%wide.region_1.0_spmd, body=%wide.region_0.0_spmd.sunk | while | flops 2000005 | bytes 3442561 | solution.py:368
  21.8 12.3 %all-to-all-start = ((f32[256,1,128]{2,1,0:T(1,128)}), f32[256,1,128]{2,1,0:T(1,128)S(1)}, u32[]{:S(2)}, u32[]{:S(2)}) async-start(f32[256,1,128]{2,1,0:T(1,128)} %bitcast.26), calls=%async_computation | async-start | bytes 262144 | tf_op jit(solution)/shard_map/while/body/eval_jaxpr/all_to_all | solution.py:322
  34.4 1.5 collective-permute-start
  35.8 2.7 %collective-permute-start.1 = (f32[32,128]{1,0:T(8,128)S(1)}, f32[32,128]{1,0:T(8,128)S(1)}, u32[]{:S(2)}, u32[]{:S(2)}) collective-permute-start(f32[32,128]{1,0:T(8,128)S(1)} %get-tuple-element.675), channel_id=1, source_target_pairs={{32,0},{64,32},{96,64},{128,96},{160,128},{192,160},{224,192},{0,2... | collective-permute-start | bytes 49160 | tf_op jit(solution)/shard_map/while/body/eval_jaxpr/ppermute | solution.py:317
  38.5 1.7 collective-permute-start.4
  40.5 2.5 %collective-permute-start.3 = (f32[16,128]{1,0:T(8,128)S(1)}, f32[16,128]{1,0:T(8,128)S(1)}, u32[]{:S(2)}, u32[]{:S(2)}) collective-permute-start(f32[16,128]{1,0:T(8,128)S(1)} %get-tuple-element.677), channel_id=1, source_target_pairs={{8,0},{16,8},{24,16},{0,24},{9,1},{17,9},{25,17},{1,25},{10,2},{18... | collective-permute-start | bytes 24584 | tf_op jit(solution)/shard_map/while/body/eval_jaxpr/ppermute | solution.py:317
  43.1 1.4 collective-permute-done.3.from_yhi
  44.5 2.2 all-to-all-done
  46.7 2.2 eval_jaxpr.10
  48.9 11.3 %all-to-all-start.1 = ((f32[256,1,128]{2,1,0:T(1,128)}), f32[256,1,128]{2,1,0:T(1,128)S(1)}, u32[]{:S(2)}, u32[]{:S(2)}) async-start(f32[256,1,128]{2,1,0:T(1,128)} %bitcast.28), calls=%async_computation.1 | async-start | bytes 262144 | tf_op jit(solution)/shard_map/while/body/eval_jaxpr/all_to_all | solution.py:322
  60.4 1.5 collective-permute-start.6
  61.8 2.7 %collective-permute-start.7 = (f32[32,128]{1,0:T(8,128)S(1)}, f32[32,128]{1,0:T(8,128)S(1)}, u32[]{:S(2)}, u32[]{:S(2)}) collective-permute-start(f32[32,128]{1,0:T(8,128)S(1)} %get-tuple-element.617), channel_id=1, source_target_pairs={{32,0},{64,32},{96,64},{128,96},{160,128},{192,160},{224,192},{0,2... | collective-permute-start | bytes 49160 | tf_op jit(solution)/shard_map/while/body/eval_jaxpr/ppermute | solution.py:317
  64.5 2.0 collective-permute-start.11
  66.5 2.5 %collective-permute-start.9 = (f32[16,128]{1,0:T(8,128)S(1)}, f32[16,128]{1,0:T(8,128)S(1)}, u32[]{:S(2)}, u32[]{:S(2)}) collective-permute-start(f32[16,128]{1,0:T(8,128)S(1)} %get-tuple-element.619), channel_id=1, source_target_pairs={{8,0},{16,8},{24,16},{0,24},{9,1},{17,9},{25,17},{1,25},{10,2},{18... | collective-permute-start | bytes 24584 | tf_op jit(solution)/shard_map/while/body/eval_jaxpr/ppermute | solution.py:317
  69.1 1.4 collective-permute-done.9.from_yhi
  71.1 1.6 all-to-all-done.1
  72.7 2.2 eval_jaxpr.11
  74.9 10.1 %all-to-all-start = ((f32[256,1,128]{2,1,0:T(1,128)}), f32[256,1,128]{2,1,0:T(1,128)S(1)}, u32[]{:S(2)}, u32[]{:S(2)}) async-start(f32[256,1,128]{2,1,0:T(1,128)} %bitcast.26), calls=%async_computation | async-start | bytes 262144 | tf_op jit(solution)/shard_map/while/body/eval_jaxpr/all_to_all | solution.py:322
  85.2 1.5 collective-permute-start
  86.6 2.7 %collective-permute-start.1 = (f32[32,128]{1,0:T(8,128)S(1)}, f32[32,128]{1,0:T(8,128)S(1)}, u32[]{:S(2)}, u32[]{:S(2)}) collective-permute-start(f32[32,128]{1,0:T(8,128)S(1)} %get-tuple-element.675), channel_id=1, source_target_pairs={{32,0},{64,32},{96,64},{128,96},{160,128},{192,160},{224,192},{0,2... | collective-permute-start | bytes 49160 | tf_op jit(solution)/shard_map/while/body/eval_jaxpr/ppermute | solution.py:317
  89.3 1.7 collective-permute-start.4
  91.3 2.5 %collective-permute-start.3 = (f32[16,128]{1,0:T(8,128)S(1)}, f32[16,128]{1,0:T(8,128)S(1)}, u32[]{:S(2)}, u32[]{:S(2)}) collective-permute-start(f32[16,128]{1,0:T(8,128)S(1)} %get-tuple-element.677), channel_id=1, source_target_pairs={{8,0},{16,8},{24,16},{0,24},{9,1},{17,9},{25,17},{1,25},{10,2},{18... | collective-permute-start | bytes 24584 | tf_op jit(solution)/shard_map/while/body/eval_jaxpr/ppermute | solution.py:317
  93.9 1.4 collective-permute-done.3.from_yhi
  95.3 2.2 all-to-all-done
  97.5 2.2 eval_jaxpr.10
  99.7 11.3 %all-to-all-start.1 = ((f32[256,1,128]{2,1,0:T(1,128)}), f32[256,1,128]{2,1,0:T(1,128)S(1)}, u32[]{:S(2)}, u32[]{:S(2)}) async-start(f32[256,1,128]{2,1,0:T(1,128)} %bitcast.28), calls=%async_computation.1 | async-start | bytes 262144 | tf_op jit(solution)/shard_map/while/body/eval_jaxpr/all_to_all | solution.py:322
  111.1 1.5 collective-permute-start.6
  112.6 2.7 %collective-permute-start.7 = (f32[32,128]{1,0:T(8,128)S(1)}, f32[32,128]{1,0:T(8,128)S(1)}, u32[]{:S(2)}, u32[]{:S(2)}) collective-permute-start(f32[32,128]{1,0:T(8,128)S(1)} %get-tuple-element.617), channel_id=1, source_target_pairs={{32,0},{64,32},{96,64},{128,96},{160,128},{192,160},{224,192},{0,2... | collective-permute-start | bytes 49160 | tf_op jit(solution)/shard_map/while/body/eval_jaxpr/ppermute | solution.py:317
  115.3 2.0 collective-permute-start.11
  117.3 2.5 %collective-permute-start.9 = (f32[16,128]{1,0:T(8,128)S(1)}, f32[16,128]{1,0:T(8,128)S(1)}, u32[]{:S(2)}, u32[]{:S(2)}) collective-permute-start(f32[16,128]{1,0:T(8,128)S(1)} %get-tuple-element.619), channel_id=1, source_target_pairs={{8,0},{16,8},{24,16},{0,24},{9,1},{17,9},{25,17},{1,25},{10,2},{18... | collective-permute-start | bytes 24584 | tf_op jit(solution)/shard_map/while/body/eval_jaxpr/ppermute | solution.py:317
  119.9 1.4 collective-permute-done.9.from_yhi
  121.9 1.6 all-to-all-done.1
  123.5 2.2 eval_jaxpr.11
  125.7 10.1 %all-to-all-start = ((f32[256,1,128]{2,1,0:T(1,128)}), f32[256,1,128]{2,1,0:T(1,128)S(1)}, u32[]{:S(2)}, u32[]{:S(2)}) async-start(f32[256,1,128]{2,1,0:T(1,128)} %bitcast.26), calls=%async_computation | async-start | bytes 262144 | tf_op jit(solution)/shard_map/while/body/eval_jaxpr/all_to_all | solution.py:322
  135.9 1.5 collective-permute-start
  137.4 2.7 %collective-permute-start.1 = (f32[32,128]{1,0:T(8,128)S(1)}, f32[32,128]{1,0:T(8,128)S(1)}, u32[]{:S(2)}, u32[]{:S(2)}) collective-permute-start(f32[32,128]{1,0:T(8,128)S(1)} %get-tuple-element.675), channel_id=1, source_target_pairs={{32,0},{64,32},{96,64},{128,96},{160,128},{192,160},{224,192},{0,2... | collective-permute-start | bytes 49160 | tf_op jit(solution)/shard_map/while/body/eval_jaxpr/ppermute | solution.py:317
  140.1 1.7 collective-permute-start.4
  142.1 2.5 %collective-permute-start.3 = (f32[16,128]{1,0:T(8,128)S(1)}, f32[16,128]{1,0:T(8,128)S(1)}, u32[]{:S(2)}, u32[]{:S(2)}) collective-permute-start(f32[16,128]{1,0:T(8,128)S(1)} %get-tuple-element.677), channel_id=1, source_target_pairs={{8,0},{16,8},{24,16},{0,24},{9,1},{17,9},{25,17},{1,25},{10,2},{18... | collective-permute-start | bytes 24584 | tf_op jit(solution)/shard_map/while/body/eval_jaxpr/ppermute | solution.py:317
  146.1 2.2 all-to-all-done
  148.3 2.2 eval_jaxpr.10
  150.5 11.3 %all-to-all-start.1 = ((f32[256,1,128]{2,1,0:T(1,128)}), f32[256,1,128]{2,1,0:T(1,128)S(1)}, u32[]{:S(2)}, u32[]{:S(2)}) async-start(f32[256,1,128]{2,1,0:T(1,128)} %bitcast.28), calls=%async_computation.1 | async-start | bytes 262144 | tf_op jit(solution)/shard_map/while/body/eval_jaxpr/all_to_all | solution.py:322
  161.9 1.5 collective-permute-start.6
  163.4 2.7 %collective-permute-start.7 = (f32[32,128]{1,0:T(8,128)S(1)}, f32[32,128]{1,0:T(8,128)S(1)}, u32[]{:S(2)}, u32[]{:S(2)}) collective-permute-start(f32[32,128]{1,0:T(8,128)S(1)} %get-tuple-element.617), channel_id=1, source_target_pairs={{32,0},{64,32},{96,64},{128,96},{160,128},{192,160},{224,192},{0,2... | collective-permute-start | bytes 49160 | tf_op jit(solution)/shard_map/while/body/eval_jaxpr/ppermute | solution.py:317
  166.1 2.0 collective-permute-start.11
  168.1 2.5 %collective-permute-start.9 = (f32[16,128]{1,0:T(8,128)S(1)}, f32[16,128]{1,0:T(8,128)S(1)}, u32[]{:S(2)}, u32[]{:S(2)}) collective-permute-start(f32[16,128]{1,0:T(8,128)S(1)} %get-tuple-element.619), channel_id=1, source_target_pairs={{8,0},{16,8},{24,16},{0,24},{9,1},{17,9},{25,17},{1,25},{10,2},{18... | collective-permute-start | bytes 24584 | tf_op jit(solution)/shard_map/while/body/eval_jaxpr/ppermute | solution.py:317
  172.6 1.6 all-to-all-done.1
  174.2 2.2 eval_jaxpr.11
  176.7 10.1 %all-to-all-start.2 = ((f32[256,1,128]{2,1,0:T(1,128)}), f32[256,1,128]{2,1,0:T(1,128)S(1)}, u32[]{:S(2)}, u32[]{:S(2)}) async-start(f32[256,1,128]{2,1,0:T(1,128)} %bitcast.8), calls=%async_computation.2 | async-start | bytes 262144 | tf_op jit(solution)/shard_map/all_to_all | solution.py:322
  186.8 2.8 %collective-permute-start.21 = (f32[16,128]{1,0:T(8,128)S(1)}, f32[16,128]{1,0:T(8,128)S(1)}, u32[]{:S(2)}, u32[]{:S(2)}) collective-permute-start(f32[16,128]{1,0:T(8,128)S(1)} %get-tuple-element.411), channel_id=1, source_target_pairs={{8,0},{16,8},{24,16},{0,24},{9,1},{17,9},{25,17},{1,25},{10,2},{18... | collective-permute-start | bytes 24584 | tf_op jit(solution)/shard_map/ppermute | solution.py:317
  189.6 2.9 %collective-permute-start.19 = (f32[32,128]{1,0:T(8,128)S(1)}, f32[32,128]{1,0:T(8,128)S(1)}, u32[]{:S(2)}, u32[]{:S(2)}) collective-permute-start(f32[32,128]{1,0:T(8,128)S(1)} %get-tuple-element.409), channel_id=1, source_target_pairs={{32,0},{64,32},{96,64},{128,96},{160,128},{192,160},{224,192},{0,2... | collective-permute-start | bytes 49160 | tf_op jit(solution)/shard_map/ppermute | solution.py:317
  192.5 1.7 collective-permute-start.22
  194.5 4.6 %collective-permute-done.20.from_ylo = f32[16,128]{1,0:T(8,128)S(1)} collective-permute-done((f32[16,128]{1,0:T(8,128)S(1)}, f32[16,128]{1,0:T(8,128)S(1)}, u32[]{:S(2)}, u32[]{:S(2)}) %collective-permute-start.20) | collective-permute-done | bytes 8224 | tf_op jit(solution)/shard_map/ppermute | solution.py:316
  199.3 2.3 shard_map.62
  201.5 26.4 %all_to_all.53 = f32[256,1,128]{2,1,0:T(1,128)S(1)} all-to-all(f32[256,1,128]{2,1,0:T(1,128)S(1)} %bitcast.35), channel_id=1, replica_groups=mesh['gx'=8,'gy'=4,'gz'=8] {'gx','gy','gz'}, dimensions={0} | all-to-all | bytes 262144 | tf_op jit(solution)/shard_map/all_to_all | solution.py:322
  228.9 6.1 %all-to-all-start.4 = ((f32[256,1,128]{2,1,0:T(1,128)}), f32[256,1,128]{2,1,0:T(1,128)S(1)}, u32[]{:S(2)}, u32[]{:S(2)}) async-start(f32[256,1,128]{2,1,0:T(1,128)} %bitcast.14), calls=%async_computation.4 | async-start | bytes 262144 | tf_op jit(solution)/shard_map/all_to_all | solution.py:322
  235.0 2.6 %shard_map.64 = f32[16,64,128]{2,1,0:T(8,128)} custom-call(f32[2,18,40,128]{3,2,1,0:T(8,128)S(1)} %get-tuple-element.429.spin), custom_call_target="tpu_custom_call" | custom-call | flops 1000000 | bytes 1000000 | tf_op jit(solution)/shard_map/pallas_call | solution.py:299
  237.6 10.0 %all-to-all-done.4 = f32[256,1,128]{2,1,0:T(1,128)S(1)} async-done(((f32[256,1,128]{2,1,0:T(1,128)}), f32[256,1,128]{2,1,0:T(1,128)S(1)}, u32[]{:S(2)}, u32[]{:S(2)}) %all-to-all-start.4) | async-done | bytes 131104 | tf_op jit(solution)/shard_map/all_to_all | solution.py:322
  (63 shorter events, 9.2 us)
Async XLA Ops:
  3.1 6.3 %collective-permute-start.14 = (f32[2,16,128]{2,1,0:T(8,128)S(1)}, f32[2,16,128]{2,1,0:T(8,128)S(1)}, u32[]{:S(2)}, u32[]{:S(2)}) collective-permute-start(f32[2,16,128]{2,1,0:T(8,128)S(1)} %get-tuple-element.384), channel_id=1, source_target_pairs={{0,8},{8,16},{16,24},{24,0},{1,9},{9,17},{17,25},{25,1},{2,10},{10... | collective-permute-start | bytes 49160 | tf_op jit(solution)/shard_map/ppermute | solution.py:316
  3.2 16.4 %collective-permute-start.12 = (f32[2,32,128]{2,1,0:T(8,128)S(1)}, f32[2,32,128]{2,1,0:T(8,128)S(1)}, u32[]{:S(2)}, u32[]{:S(2)}) collective-permute-start(f32[2,32,128]{2,1,0:T(8,128)S(1)} %get-tuple-element.382), channel_id=1, source_target_pairs={{0,32},{32,64},{64,96},{96,128},{128,160},{160,192},{192,224},{224... | collective-permute-start | bytes 98312 | tf_op jit(solution)/shard_map/ppermute | solution.py:316
  4.8 14.9 %collective-permute-start.13 = (f32[2,32,128]{2,1,0:T(8,128)S(1)}, f32[2,32,128]{2,1,0:T(8,128)S(1)}, u32[]{:S(2)}, u32[]{:S(2)}) collective-permute-start(f32[2,32,128]{2,1,0:T(8,128)S(1)} %get-tuple-element.383), channel_id=1, source_target_pairs={{32,0},{64,32},{96,64},{128,96},{160,128},{192,160},{224,192},{0,2... | collective-permute-start | bytes 98312 | tf_op jit(solution)/shard_map/ppermute | solution.py:317
  7.4 12.2 %collective-permute-start.17 = (f32[2,32,128]{2,1,0:T(8,128)S(1)}, f32[2,32,128]{2,1,0:T(8,128)S(1)}, u32[]{:S(2)}, u32[]{:S(2)}) collective-permute-start(f32[2,32,128]{2,1,0:T(8,128)S(1)} %get-tuple-element.386), channel_id=1, source_target_pairs={{1,0},{2,1},{3,2},{4,3},{5,4},{6,5},{7,6},{0,7},{9,8},{10,9},{11,1... | collective-permute-start | bytes 98312 | tf_op jit(solution)/shard_map/ppermute | solution.py:317
  9.2 10.4 %collective-permute-start.16 = (f32[2,32,128]{2,1,0:T(8,128)S(1)}, f32[2,32,128]{2,1,0:T(8,128)S(1)}, u32[]{:S(2)}, u32[]{:S(2)}) collective-permute-start(f32[2,32,128]{2,1,0:T(8,128)S(1)} %get-tuple-element.386), channel_id=1, source_target_pairs={{0,1},{1,2},{2,3},{3,4},{4,5},{5,6},{6,7},{7,0},{8,9},{9,10},{10,1... | collective-permute-start | bytes 98312 | tf_op jit(solution)/shard_map/ppermute | solution.py:316
  9.4 10.2 %collective-permute-start.15 = (f32[2,16,128]{2,1,0:T(8,128)S(1)}, f32[2,16,128]{2,1,0:T(8,128)S(1)}, u32[]{:S(2)}, u32[]{:S(2)}) collective-permute-start(f32[2,16,128]{2,1,0:T(8,128)S(1)} %get-tuple-element.385), channel_id=1, source_target_pairs={{8,0},{16,8},{24,16},{0,24},{9,1},{17,9},{25,17},{1,25},{10,2},{18... | collective-permute-start | bytes 49160 | tf_op jit(solution)/shard_map/ppermute | solution.py:317
  21.8 24.8 %all-to-all-start = ((f32[256,1,128]{2,1,0:T(1,128)}), f32[256,1,128]{2,1,0:T(1,128)S(1)}, u32[]{:S(2)}, u32[]{:S(2)}) async-start(f32[256,1,128]{2,1,0:T(1,128)} %bitcast.26), calls=%async_computation | async-start | bytes 262144 | tf_op jit(solution)/shard_map/while/body/eval_jaxpr/all_to_all | solution.py:322
  34.2 6.4 %collective-permute-start.2 = (f32[16,128]{1,0:T(8,128)S(1)}, f32[16,128]{1,0:T(8,128)S(1)}, u32[]{:S(2)}, u32[]{:S(2)}) collective-permute-start(f32[16,128]{1,0:T(8,128)S(1)} %get-tuple-element.678), channel_id=1, source_target_pairs={{0,8},{8,16},{16,24},{24,0},{1,9},{9,17},{17,25},{25,1},{2,10},{10... | collective-permute-start | bytes 24584 | tf_op jit(solution)/shard_map/while/body/eval_jaxpr/ppermute | solution.py:316
  34.4 10.1 %collective-permute-start = (f32[32,128]{1,0:T(8,128)S(1)}, f32[32,128]{1,0:T(8,128)S(1)}, u32[]{:S(2)}, u32[]{:S(2)}) collective-permute-start(f32[32,128]{1,0:T(8,128)S(1)} %get-tuple-element.676), channel_id=1, source_target_pairs={{0,32},{32,64},{64,96},{96,128},{128,160},{160,192},{192,224},{224... | collective-permute-start | bytes 49160 | tf_op jit(solution)/shard_map/while/body/eval_jaxpr/ppermute | solution.py:316
  35.8 8.6 %collective-permute-start.1 = (f32[32,128]{1,0:T(8,128)S(1)}, f32[32,128]{1,0:T(8,128)S(1)}, u32[]{:S(2)}, u32[]{:S(2)}) collective-permute-start(f32[32,128]{1,0:T(8,128)S(1)} %get-tuple-element.675), channel_id=1, source_target_pairs={{32,0},{64,32},{96,64},{128,96},{160,128},{192,160},{224,192},{0,2... | collective-permute-start | bytes 49160 | tf_op jit(solution)/shard_map/while/body/eval_jaxpr/ppermute | solution.py:317
  38.5 6.0 %collective-permute-start.4 = (f32[32,128]{1,0:T(8,128)S(1)}, f32[32,128]{1,0:T(8,128)S(1)}, u32[]{:S(2)}, u32[]{:S(2)}) collective-permute-start(f32[32,128]{1,0:T(8,128)S(1)} %get-tuple-element.679), channel_id=1, source_target_pairs={{0,1},{1,2},{2,3},{3,4},{4,5},{5,6},{6,7},{7,0},{8,9},{9,10},{10,1... | collective-permute-start | bytes 49160 | tf_op jit(solution)/shard_map/while/body/eval_jaxpr/ppermute | solution.py:316
  40.2 4.2 %collective-permute-start.5 = (f32[32,128]{1,0:T(8,128)S(1)}, f32[32,128]{1,0:T(8,128)S(1)}, u32[]{:S(2)}, u32[]{:S(2)}) collective-permute-start(f32[32,128]{1,0:T(8,128)S(1)} %get-tuple-element.679), channel_id=1, source_target_pairs={{1,0},{2,1},{3,2},{4,3},{5,4},{6,5},{7,6},{0,7},{9,8},{10,9},{11,1... | collective-permute-start | bytes 49160 | tf_op jit(solution)/shard_map/while/body/eval_jaxpr/ppermute | solution.py:317
  40.5 3.9 %collective-permute-start.3 = (f32[16,128]{1,0:T(8,128)S(1)}, f32[16,128]{1,0:T(8,128)S(1)}, u32[]{:S(2)}, u32[]{:S(2)}) collective-permute-start(f32[16,128]{1,0:T(8,128)S(1)} %get-tuple-element.677), channel_id=1, source_target_pairs={{8,0},{16,8},{24,16},{0,24},{9,1},{17,9},{25,17},{1,25},{10,2},{18... | collective-permute-start | bytes 24584 | tf_op jit(solution)/shard_map/while/body/eval_jaxpr/ppermute | solution.py:317
  48.9 23.8 %all-to-all-start.1 = ((f32[256,1,128]{2,1,0:T(1,128)}), f32[256,1,128]{2,1,0:T(1,128)S(1)}, u32[]{:S(2)}, u32[]{:S(2)}) async-start(f32[256,1,128]{2,1,0:T(1,128)} %bitcast.28), calls=%async_computation.1 | async-start | bytes 262144 | tf_op jit(solution)/shard_map/while/body/eval_jaxpr/all_to_all | solution.py:322
  60.2 6.4 %collective-permute-start.8 = (f32[16,128]{1,0:T(8,128)S(1)}, f32[16,128]{1,0:T(8,128)S(1)}, u32[]{:S(2)}, u32[]{:S(2)}) collective-permute-start(f32[16,128]{1,0:T(8,128)S(1)} %get-tuple-element.618), channel_id=1, source_target_pairs={{0,8},{8,16},{16,24},{24,0},{1,9},{9,17},{17,25},{25,1},{2,10},{10... | collective-permute-start | bytes 24584 | tf_op jit(solution)/shard_map/while/body/eval_jaxpr/ppermute | solution.py:316
  60.4 10.1 %collective-permute-start.6 = (f32[32,128]{1,0:T(8,128)S(1)}, f32[32,128]{1,0:T(8,128)S(1)}, u32[]{:S(2)}, u32[]{:S(2)}) collective-permute-start(f32[32,128]{1,0:T(8,128)S(1)} %get-tuple-element.616), channel_id=1, source_target_pairs={{0,32},{32,64},{64,96},{96,128},{128,160},{160,192},{192,224},{224... | collective-permute-start | bytes 49160 | tf_op jit(solution)/shard_map/while/body/eval_jaxpr/ppermute | solution.py:316
  61.8 8.6 %collective-permute-start.7 = (f32[32,128]{1,0:T(8,128)S(1)}, f32[32,128]{1,0:T(8,128)S(1)}, u32[]{:S(2)}, u32[]{:S(2)}) collective-permute-start(f32[32,128]{1,0:T(8,128)S(1)} %get-tuple-element.617), channel_id=1, source_target_pairs={{32,0},{64,32},{96,64},{128,96},{160,128},{192,160},{224,192},{0,2... | collective-permute-start | bytes 49160 | tf_op jit(solution)/shard_map/while/body/eval_jaxpr/ppermute | solution.py:317
  64.5 6.0 %collective-permute-start.11 = (f32[32,128]{1,0:T(8,128)S(1)}, f32[32,128]{1,0:T(8,128)S(1)}, u32[]{:S(2)}, u32[]{:S(2)}) collective-permute-start(f32[32,128]{1,0:T(8,128)S(1)} %get-tuple-element.620), channel_id=1, source_target_pairs={{1,0},{2,1},{3,2},{4,3},{5,4},{6,5},{7,6},{0,7},{9,8},{10,9},{11,1... | collective-permute-start | bytes 49160 | tf_op jit(solution)/shard_map/while/body/eval_jaxpr/ppermute | solution.py:317
  66.5 4.6 %collective-permute-start.10 = (f32[32,128]{1,0:T(8,128)S(1)}, f32[32,128]{1,0:T(8,128)S(1)}, u32[]{:S(2)}, u32[]{:S(2)}) collective-permute-start(f32[32,128]{1,0:T(8,128)S(1)} %get-tuple-element.620), channel_id=1, source_target_pairs={{0,1},{1,2},{2,3},{3,4},{4,5},{5,6},{6,7},{7,0},{8,9},{9,10},{10,1... | collective-permute-start | bytes 49160 | tf_op jit(solution)/shard_map/while/body/eval_jaxpr/ppermute | solution.py:316
  66.5 3.9 %collective-permute-start.9 = (f32[16,128]{1,0:T(8,128)S(1)}, f32[16,128]{1,0:T(8,128)S(1)}, u32[]{:S(2)}, u32[]{:S(2)}) collective-permute-start(f32[16,128]{1,0:T(8,128)S(1)} %get-tuple-element.619), channel_id=1, source_target_pairs={{8,0},{16,8},{24,16},{0,24},{9,1},{17,9},{25,17},{1,25},{10,2},{18... | collective-permute-start | bytes 24584 | tf_op jit(solution)/shard_map/while/body/eval_jaxpr/ppermute | solution.py:317
  74.9 22.6 %all-to-all-start = ((f32[256,1,128]{2,1,0:T(1,128)}), f32[256,1,128]{2,1,0:T(1,128)S(1)}, u32[]{:S(2)}, u32[]{:S(2)}) async-start(f32[256,1,128]{2,1,0:T(1,128)} %bitcast.26), calls=%async_computation | async-start | bytes 262144 | tf_op jit(solution)/shard_map/while/body/eval_jaxpr/all_to_all | solution.py:322
  85.0 6.4 %collective-permute-start.2 = (f32[16,128]{1,0:T(8,128)S(1)}, f32[16,128]{1,0:T(8,128)S(1)}, u32[]{:S(2)}, u32[]{:S(2)}) collective-permute-start(f32[16,128]{1,0:T(8,128)S(1)} %get-tuple-element.678), channel_id=1, source_target_pairs={{0,8},{8,16},{16,24},{24,0},{1,9},{9,17},{17,25},{25,1},{2,10},{10... | collective-permute-start | bytes 24584 | tf_op jit(solution)/shard_map/while/body/eval_jaxpr/ppermute | solution.py:316
  85.2 10.1 %collective-permute-start = (f32[32,128]{1,0:T(8,128)S(1)}, f32[32,128]{1,0:T(8,128)S(1)}, u32[]{:S(2)}, u32[]{:S(2)}) collective-permute-start(f32[32,128]{1,0:T(8,128)S(1)} %get-tuple-element.676), channel_id=1, source_target_pairs={{0,32},{32,64},{64,96},{96,128},{128,160},{160,192},{192,224},{224... | collective-permute-start | bytes 49160 | tf_op jit(solution)/shard_map/while/body/eval_jaxpr/ppermute | solution.py:316
  86.6 8.6 %collective-permute-start.1 = (f32[32,128]{1,0:T(8,128)S(1)}, f32[32,128]{1,0:T(8,128)S(1)}, u32[]{:S(2)}, u32[]{:S(2)}) collective-permute-start(f32[32,128]{1,0:T(8,128)S(1)} %get-tuple-element.675), channel_id=1, source_target_pairs={{32,0},{64,32},{96,64},{128,96},{160,128},{192,160},{224,192},{0,2... | collective-permute-start | bytes 49160 | tf_op jit(solution)/shard_map/while/body/eval_jaxpr/ppermute | solution.py:317
  89.3 6.0 %collective-permute-start.4 = (f32[32,128]{1,0:T(8,128)S(1)}, f32[32,128]{1,0:T(8,128)S(1)}, u32[]{:S(2)}, u32[]{:S(2)}) collective-permute-start(f32[32,128]{1,0:T(8,128)S(1)} %get-tuple-element.679), channel_id=1, source_target_pairs={{0,1},{1,2},{2,3},{3,4},{4,5},{5,6},{6,7},{7,0},{8,9},{9,10},{10,1... | collective-permute-start | bytes 49160 | tf_op jit(solution)/shard_map/while/body/eval_jaxpr/ppermute | solution.py:316
  91.0 4.2 %collective-permute-start.5 = (f32[32,128]{1,0:T(8,128)S(1)}, f32[32,128]{1,0:T(8,128)S(1)}, u32[]{:S(2)}, u32[]{:S(2)}) collective-permute-start(f32[32,128]{1,0:T(8,128)S(1)} %get-tuple-element.679), channel_id=1, source_target_pairs={{1,0},{2,1},{3,2},{4,3},{5,4},{6,5},{7,6},{0,7},{9,8},{10,9},{11,1... | collective-permute-start | bytes 49160 | tf_op jit(solution)/shard_map/while/body/eval_jaxpr/ppermute | solution.py:317
  91.3 3.9 %collective-permute-start.3 = (f32[16,128]{1,0:T(8,128)S(1)}, f32[16,128]{1,0:T(8,128)S(1)}, u32[]{:S(2)}, u32[]{:S(2)}) collective-permute-start(f32[16,128]{1,0:T(8,128)S(1)} %get-tuple-element.677), channel_id=1, source_target_pairs={{8,0},{16,8},{24,16},{0,24},{9,1},{17,9},{25,17},{1,25},{10,2},{18... | collective-permute-start | bytes 24584 | tf_op jit(solution)/shard_map/while/body/eval_jaxpr/ppermute | solution.py:317
  99.7 23.8 %all-to-all-start.1 = ((f32[256,1,128]{2,1,0:T(1,128)}), f32[256,1,128]{2,1,0:T(1,128)S(1)}, u32[]{:S(2)}, u32[]{:S(2)}) async-start(f32[256,1,128]{2,1,0:T(1,128)} %bitcast.28), calls=%async_computation.1 | async-start | bytes 262144 | tf_op jit(solution)/shard_map/while/body/eval_jaxpr/all_to_all | solution.py:322
  110.9 6.4 %collective-permute-start.8 = (f32[16,128]{1,0:T(8,128)S(1)}, f32[16,128]{1,0:T(8,128)S(1)}, u32[]{:S(2)}, u32[]{:S(2)}) collective-permute-start(f32[16,128]{1,0:T(8,128)S(1)} %get-tuple-element.618), channel_id=1, source_target_pairs={{0,8},{8,16},{16,24},{24,0},{1,9},{9,17},{17,25},{25,1},{2,10},{10... | collective-permute-start | bytes 24584 | tf_op jit(solution)/shard_map/while/body/eval_jaxpr/ppermute | solution.py:316
  111.1 10.1 %collective-permute-start.6 = (f32[32,128]{1,0:T(8,128)S(1)}, f32[32,128]{1,0:T(8,128)S(1)}, u32[]{:S(2)}, u32[]{:S(2)}) collective-permute-start(f32[32,128]{1,0:T(8,128)S(1)} %get-tuple-element.616), channel_id=1, source_target_pairs={{0,32},{32,64},{64,96},{96,128},{128,160},{160,192},{192,224},{224... | collective-permute-start | bytes 49160 | tf_op jit(solution)/shard_map/while/body/eval_jaxpr/ppermute | solution.py:316
  112.6 8.6 %collective-permute-start.7 = (f32[32,128]{1,0:T(8,128)S(1)}, f32[32,128]{1,0:T(8,128)S(1)}, u32[]{:S(2)}, u32[]{:S(2)}) collective-permute-start(f32[32,128]{1,0:T(8,128)S(1)} %get-tuple-element.617), channel_id=1, source_target_pairs={{32,0},{64,32},{96,64},{128,96},{160,128},{192,160},{224,192},{0,2... | collective-permute-start | bytes 49160 | tf_op jit(solution)/shard_map/while/body/eval_jaxpr/ppermute | solution.py:317
  115.3 6.0 %collective-permute-start.11 = (f32[32,128]{1,0:T(8,128)S(1)}, f32[32,128]{1,0:T(8,128)S(1)}, u32[]{:S(2)}, u32[]{:S(2)}) collective-permute-start(f32[32,128]{1,0:T(8,128)S(1)} %get-tuple-element.620), channel_id=1, source_target_pairs={{1,0},{2,1},{3,2},{4,3},{5,4},{6,5},{7,6},{0,7},{9,8},{10,9},{11,1... | collective-permute-start | bytes 49160 | tf_op jit(solution)/shard_map/while/body/eval_jaxpr/ppermute | solution.py:317
  117.3 4.6 %collective-permute-start.10 = (f32[32,128]{1,0:T(8,128)S(1)}, f32[32,128]{1,0:T(8,128)S(1)}, u32[]{:S(2)}, u32[]{:S(2)}) collective-permute-start(f32[32,128]{1,0:T(8,128)S(1)} %get-tuple-element.620), channel_id=1, source_target_pairs={{0,1},{1,2},{2,3},{3,4},{4,5},{5,6},{6,7},{7,0},{8,9},{9,10},{10,1... | collective-permute-start | bytes 49160 | tf_op jit(solution)/shard_map/while/body/eval_jaxpr/ppermute | solution.py:316
  117.3 3.9 %collective-permute-start.9 = (f32[16,128]{1,0:T(8,128)S(1)}, f32[16,128]{1,0:T(8,128)S(1)}, u32[]{:S(2)}, u32[]{:S(2)}) collective-permute-start(f32[16,128]{1,0:T(8,128)S(1)} %get-tuple-element.619), channel_id=1, source_target_pairs={{8,0},{16,8},{24,16},{0,24},{9,1},{17,9},{25,17},{1,25},{10,2},{18... | collective-permute-start | bytes 24584 | tf_op jit(solution)/shard_map/while/body/eval_jaxpr/ppermute | solution.py:317
  125.7 22.6 %all-to-all-start = ((f32[256,1,128]{2,1,0:T(1,128)}), f32[256,1,128]{2,1,0:T(1,128)S(1)}, u32[]{:S(2)}, u32[]{:S(2)}) async-start(f32[256,1,128]{2,1,0:T(1,128)} %bitcast.26), calls=%async_computation | async-start | bytes 262144 | tf_op jit(solution)/shard_map/while/body/eval_jaxpr/all_to_all | solution.py:322
  135.7 6.4 %collective-permute-start.2 = (f32[16,128]{1,0:T(8,128)S(1)}, f32[16,128]{1,0:T(8,128)S(1)}, u32[]{:S(2)}, u32[]{:S(2)}) collective-permute-start(f32[16,128]{1,0:T(8,128)S(1)} %get-tuple-element.678), channel_id=1, source_target_pairs={{0,8},{8,16},{16,24},{24,0},{1,9},{9,17},{17,25},{25,1},{2,10},{10... | collective-permute-start | bytes 24584 | tf_op jit(solution)/shard_map/while/body/eval_jaxpr/ppermute | solution.py:316
  135.9 10.1 %collective-permute-start = (f32[32,128]{1,0:T(8,128)S(1)}, f32[32,128]{1,0:T(8,128)S(1)}, u32[]{:S(2)}, u32[]{:S(2)}) collective-permute-start(f32[32,128]{1,0:T(8,128)S(1)} %get-tuple-element.676), channel_id=1, source_target_pairs={{0,32},{32,64},{64,96},{96,128},{128,160},{160,192},{192,224},{224... | collective-permute-start | bytes 49160 | tf_op jit(solution)/shard_map/while/body/eval_jaxpr/ppermute | solution.py:316
  137.4 8.6 %collective-permute-start.1 = (f32[32,128]{1,0:T(8,128)S(1)}, f32[32,128]{1,0:T(8,128)S(1)}, u32[]{:S(2)}, u32[]{:S(2)}) collective-permute-start(f32[32,128]{1,0:T(8,128)S(1)} %get-tuple-element.675), channel_id=1, source_target_pairs={{32,0},{64,32},{96,64},{128,96},{160,128},{192,160},{224,192},{0,2... | collective-permute-start | bytes 49160 | tf_op jit(solution)/shard_map/while/body/eval_jaxpr/ppermute | solution.py:317
  140.1 6.0 %collective-permute-start.4 = (f32[32,128]{1,0:T(8,128)S(1)}, f32[32,128]{1,0:T(8,128)S(1)}, u32[]{:S(2)}, u32[]{:S(2)}) collective-permute-start(f32[32,128]{1,0:T(8,128)S(1)} %get-tuple-element.679), channel_id=1, source_target_pairs={{0,1},{1,2},{2,3},{3,4},{4,5},{5,6},{6,7},{7,0},{8,9},{9,10},{10,1... | collective-permute-start | bytes 49160 | tf_op jit(solution)/shard_map/while/body/eval_jaxpr/ppermute | solution.py:316
  141.8 4.2 %collective-permute-start.5 = (f32[32,128]{1,0:T(8,128)S(1)}, f32[32,128]{1,0:T(8,128)S(1)}, u32[]{:S(2)}, u32[]{:S(2)}) collective-permute-start(f32[32,128]{1,0:T(8,128)S(1)} %get-tuple-element.679), channel_id=1, source_target_pairs={{1,0},{2,1},{3,2},{4,3},{5,4},{6,5},{7,6},{0,7},{9,8},{10,9},{11,1... | collective-permute-start | bytes 49160 | tf_op jit(solution)/shard_map/while/body/eval_jaxpr/ppermute | solution.py:317
  142.1 3.9 %collective-permute-start.3 = (f32[16,128]{1,0:T(8,128)S(1)}, f32[16,128]{1,0:T(8,128)S(1)}, u32[]{:S(2)}, u32[]{:S(2)}) collective-permute-start(f32[16,128]{1,0:T(8,128)S(1)} %get-tuple-element.677), channel_id=1, source_target_pairs={{8,0},{16,8},{24,16},{0,24},{9,1},{17,9},{25,17},{1,25},{10,2},{18... | collective-permute-start | bytes 24584 | tf_op jit(solution)/shard_map/while/body/eval_jaxpr/ppermute | solution.py:317
  150.5 23.8 %all-to-all-start.1 = ((f32[256,1,128]{2,1,0:T(1,128)}), f32[256,1,128]{2,1,0:T(1,128)S(1)}, u32[]{:S(2)}, u32[]{:S(2)}) async-start(f32[256,1,128]{2,1,0:T(1,128)} %bitcast.28), calls=%async_computation.1 | async-start | bytes 262144 | tf_op jit(solution)/shard_map/while/body/eval_jaxpr/all_to_all | solution.py:322
  161.7 6.4 %collective-permute-start.8 = (f32[16,128]{1,0:T(8,128)S(1)}, f32[16,128]{1,0:T(8,128)S(1)}, u32[]{:S(2)}, u32[]{:S(2)}) collective-permute-start(f32[16,128]{1,0:T(8,128)S(1)} %get-tuple-element.618), channel_id=1, source_target_pairs={{0,8},{8,16},{16,24},{24,0},{1,9},{9,17},{17,25},{25,1},{2,10},{10... | collective-permute-start | bytes 24584 | tf_op jit(solution)/shard_map/while/body/eval_jaxpr/ppermute | solution.py:316
  161.9 10.1 %collective-permute-start.6 = (f32[32,128]{1,0:T(8,128)S(1)}, f32[32,128]{1,0:T(8,128)S(1)}, u32[]{:S(2)}, u32[]{:S(2)}) collective-permute-start(f32[32,128]{1,0:T(8,128)S(1)} %get-tuple-element.616), channel_id=1, source_target_pairs={{0,32},{32,64},{64,96},{96,128},{128,160},{160,192},{192,224},{224... | collective-permute-start | bytes 49160 | tf_op jit(solution)/shard_map/while/body/eval_jaxpr/ppermute | solution.py:316
  163.4 8.6 %collective-permute-start.7 = (f32[32,128]{1,0:T(8,128)S(1)}, f32[32,128]{1,0:T(8,128)S(1)}, u32[]{:S(2)}, u32[]{:S(2)}) collective-permute-start(f32[32,128]{1,0:T(8,128)S(1)} %get-tuple-element.617), channel_id=1, source_target_pairs={{32,0},{64,32},{96,64},{128,96},{160,128},{192,160},{224,192},{0,2... | collective-permute-start | bytes 49160 | tf_op jit(solution)/shard_map/while/body/eval_jaxpr/ppermute | solution.py:317
  166.1 6.0 %collective-permute-start.11 = (f32[32,128]{1,0:T(8,128)S(1)}, f32[32,128]{1,0:T(8,128)S(1)}, u32[]{:S(2)}, u32[]{:S(2)}) collective-permute-start(f32[32,128]{1,0:T(8,128)S(1)} %get-tuple-element.620), channel_id=1, source_target_pairs={{1,0},{2,1},{3,2},{4,3},{5,4},{6,5},{7,6},{0,7},{9,8},{10,9},{11,1... | collective-permute-start | bytes 49160 | tf_op jit(solution)/shard_map/while/body/eval_jaxpr/ppermute | solution.py:317
  168.1 4.6 %collective-permute-start.10 = (f32[32,128]{1,0:T(8,128)S(1)}, f32[32,128]{1,0:T(8,128)S(1)}, u32[]{:S(2)}, u32[]{:S(2)}) collective-permute-start(f32[32,128]{1,0:T(8,128)S(1)} %get-tuple-element.620), channel_id=1, source_target_pairs={{0,1},{1,2},{2,3},{3,4},{4,5},{5,6},{6,7},{7,0},{8,9},{9,10},{10,1... | collective-permute-start | bytes 49160 | tf_op jit(solution)/shard_map/while/body/eval_jaxpr/ppermute | solution.py:316
  168.1 3.9 %collective-permute-start.9 = (f32[16,128]{1,0:T(8,128)S(1)}, f32[16,128]{1,0:T(8,128)S(1)}, u32[]{:S(2)}, u32[]{:S(2)}) collective-permute-start(f32[16,128]{1,0:T(8,128)S(1)} %get-tuple-element.619), channel_id=1, source_target_pairs={{8,0},{16,8},{24,16},{0,24},{9,1},{17,9},{25,17},{1,25},{10,2},{18... | collective-permute-start | bytes 24584 | tf_op jit(solution)/shard_map/while/body/eval_jaxpr/ppermute | solution.py:317
  176.7 22.6 %all-to-all-start.2 = ((f32[256,1,128]{2,1,0:T(1,128)}), f32[256,1,128]{2,1,0:T(1,128)S(1)}, u32[]{:S(2)}, u32[]{:S(2)}) async-start(f32[256,1,128]{2,1,0:T(1,128)} %bitcast.8), calls=%async_computation.2 | async-start | bytes 262144 | tf_op jit(solution)/shard_map/all_to_all | solution.py:322
  186.8 7.7 %collective-permute-start.21 = (f32[16,128]{1,0:T(8,128)S(1)}, f32[16,128]{1,0:T(8,128)S(1)}, u32[]{:S(2)}, u32[]{:S(2)}) collective-permute-start(f32[16,128]{1,0:T(8,128)S(1)} %get-tuple-element.411), channel_id=1, source_target_pairs={{8,0},{16,8},{24,16},{0,24},{9,1},{17,9},{25,17},{1,25},{10,2},{18... | collective-permute-start | bytes 24584 | tf_op jit(solution)/shard_map/ppermute | solution.py:317
  189.6 9.5 %collective-permute-start.19 = (f32[32,128]{1,0:T(8,128)S(1)}, f32[32,128]{1,0:T(8,128)S(1)}, u32[]{:S(2)}, u32[]{:S(2)}) collective-permute-start(f32[32,128]{1,0:T(8,128)S(1)} %get-tuple-element.409), channel_id=1, source_target_pairs={{32,0},{64,32},{96,64},{128,96},{160,128},{192,160},{224,192},{0,2... | collective-permute-start | bytes 49160 | tf_op jit(solution)/shard_map/ppermute | solution.py:317
  192.5 6.6 %collective-permute-start.18 = (f32[32,128]{1,0:T(8,128)S(1)}, f32[32,128]{1,0:T(8,128)S(1)}, u32[]{:S(2)}, u32[]{:S(2)}) collective-permute-start(f32[32,128]{1,0:T(8,128)S(1)} %get-tuple-element.408), channel_id=1, source_target_pairs={{0,32},{32,64},{64,96},{96,128},{128,160},{160,192},{192,224},{224... | collective-permute-start | bytes 49160 | tf_op jit(solution)/shard_map/ppermute | solution.py:316
  192.5 6.6 %collective-permute-start.22 = (f32[32,128]{1,0:T(8,128)S(1)}, f32[32,128]{1,0:T(8,128)S(1)}, u32[]{:S(2)}, u32[]{:S(2)}) collective-permute-start(f32[32,128]{1,0:T(8,128)S(1)} %get-tuple-element.412), channel_id=1, source_target_pairs={{0,1},{1,2},{2,3},{3,4},{4,5},{5,6},{6,7},{7,0},{8,9},{9,10},{10,1... | collective-permute-start | bytes 49160 | tf_op jit(solution)/shard_map/ppermute | solution.py:316
  194.2 4.9 %collective-permute-start.23 = (f32[32,128]{1,0:T(8,128)S(1)}, f32[32,128]{1,0:T(8,128)S(1)}, u32[]{:S(2)}, u32[]{:S(2)}) collective-permute-start(f32[32,128]{1,0:T(8,128)S(1)} %get-tuple-element.412), channel_id=1, source_target_pairs={{1,0},{2,1},{3,2},{4,3},{5,4},{6,5},{7,6},{0,7},{9,8},{10,9},{11,1... | collective-permute-start | bytes 49160 | tf_op jit(solution)/shard_map/ppermute | solution.py:317
  194.5 4.6 %collective-permute-start.20 = (f32[16,128]{1,0:T(8,128)S(1)}, f32[16,128]{1,0:T(8,128)S(1)}, u32[]{:S(2)}, u32[]{:S(2)}) collective-permute-start(f32[16,128]{1,0:T(8,128)S(1)} %get-tuple-element.410), channel_id=1, source_target_pairs={{0,8},{8,16},{16,24},{24,0},{1,9},{9,17},{17,25},{25,1},{2,10},{10... | collective-permute-start | bytes 24584 | tf_op jit(solution)/shard_map/ppermute | solution.py:316
  228.9 18.7 %all-to-all-start.4 = ((f32[256,1,128]{2,1,0:T(1,128)}), f32[256,1,128]{2,1,0:T(1,128)S(1)}, u32[]{:S(2)}, u32[]{:S(2)}) async-start(f32[256,1,128]{2,1,0:T(1,128)} %bitcast.14), calls=%async_computation.4 | async-start | bytes 262144 | tf_op jit(solution)/shard_map/all_to_all | solution.py:322
where the time goes:
time: 250 us; the launch traced here: 248 us
  starting transfers between devices  153 us (61%)
  waiting for transfers between devices  36.2 us (14%)
  Pallas kernels  31.3 us (13%)
  blocking collectives  26.4 us (11%)
    all_to_all x8, starting transfers between devices, spread(): return lax.all_to_all(sent, AXES, 0, 0, tiled=True)  82.4 us
    ppermute x24, starting transfers between devices, swap(): got.append(lax.ppermute(low, axis, [(b, a) for a, b in up]))  51.4 us
    pallas_call x13, Pallas kernels, call(): pl.pallas_call(kernel, out_shape=[pltpu.HBM(shape, F32) if i in far_out e...  31.3 us
    all_to_all x1, blocking collectives, spread(): return lax.all_to_all(sent, AXES, 0, 0, tiled=True)  26.4 us
    all_to_all x8, waiting for transfers between devices, spread(): return lax.all_to_all(sent, AXES, 0, 0, tiled=True)  21.5 us
    ppermute x24, starting transfers between devices, swap(): got.append(lax.ppermute(high, axis, up))  19 us
    ppermute x24, waiting for transfers between devices, swap(): got.append(lax.ppermute(low, axis, [(b, a) for a, b in up]))  8.25 us
    ppermute x24, waiting for transfers between devices, swap(): got.append(lax.ppermute(high, axis, up))  6.46 us
  transfers between devices with their start and end apart: 56, of which 18 were waited for; matrix products, arithmetic and copies ran while one was open for 0% of the time, Pallas kernels for 4%

commit v1 on v0

--- a/solution.py
+++ b/solution.py
@@ -42,9 +42,9 @@
     return jnp.dot(a, b, precision=precision, preferred_element_type=F32)
 
 
-def face_column(plane, x, phase):
-    ends = jnp.where(odd_row(x + phase), roll(plane, HZ + 1), plane)
-    return roll(ends, x)
+def add_face(column, plane, x, odd):
+    slot = (2 * x - jnp.where(odd, 1, 0)) % HZ
+    return jnp.where(lane_of() % HZ == slot, pltpu.roll(plane, 2 * x, 1), column)
 
 
 def fetch(pairs, arrived):
@@ -62,7 +62,7 @@
     return even_site, odd_site
 
 
-def spins_kernel(occ_hbm, spin, xlo, xhi, ylo, yhi, zed, occ, arrived):
+def spins_kernel(where, occ_hbm, spin, x_one, x_two, y_one, y_two, zed, occ, arrived):
     copies = fetch([(occ_hbm.at[pl.ds(c * CHUNK, CHUNK)], occ.at[pl.ds(c * CHUNK, CHUNK)]) for c in range(BX // CHUNK)], arrived)
     lane = lane_of()
     wide = shuffle_matrix(False)
@@ -73,14 +73,10 @@
         planes = split_sites(matmul(2.0 * occ[x].astype(F32) - 1.0, wide, False), odd_row(x), lane < HZ)
         for p, plane in enumerate(planes):
             spin[p, x + 1, :HY] = plane
-            ylo[p, x : x + 1] = plane[:1]
-            yhi[p, x : x + 1] = plane[HY - 1 :]
-            columns[p] = jnp.where(lane % HZ == x, face_column(plane, x, p), columns[p])
-            if x == 0:
-                xlo[p] = plane
-            if x == BX - 1:
-                xhi[p] = plane
+            y_one[p, x : x + 1], y_two[p, x : x + 1] = sort_faces(where[2], plane[:1], plane[HY - 1 :])
+            columns[p] = add_face(columns[p], plane, x, odd_row(x + p))
     for p in range(2):
+        x_one[p], x_two[p] = sort_faces(where[1], spin[p, 1, :HY], spin[p, BX, :HY])
         zed[p] = columns[p]
 
 
@@ -135,10 +131,21 @@
         write.wait()
 
 
-def z_parts(phase):
-    lane = lane_of()
-    row = lax.broadcasted_iota(jnp.int32, (HY, BZ), 0)
-    return (lane % HZ + row + phase) % 2 == 1
+def sort_halo(even, first, second):
+    even = even == 1
+    return jnp.where(even, second, first), jnp.where(even, first, second)
+
+
+def sort_faces(where, low, high):
+    even = where == 1
+    return jnp.where(even, high, low), jnp.where(even, low, high)
+
+
+def halo_parts(where, x_one, x_two, y_one, y_two, z_one, z_two):
+    low_x, high_x = sort_halo(where[1], x_one, x_two)
+    low_y, high_y = sort_halo(where[2], y_one, y_two)
+    low_z, high_z = sort_halo(where[3], z_one, z_two)
+    return low_x, high_x, jnp.where(lane_of(BX) < HZ, high_y, low_y), jnp.where(lane_of() % 2 == 1, low_z, high_z)
 
 
 def flip_of(total, half):
@@ -175,14 +182,14 @@
     energy[k - 1] = -eighth(of_gain) - fields[1 - p]
     if halo is None:
         return
-    from_xlo, from_xhi, from_ylo, from_yhi, from_zlo, from_zhi = halo
-    spin[p, 0, :HY] = spin[p, 0, :HY] * flip(from_xlo[...])
-    spin[p, BX + 1, :HY] = spin[p, BX + 1, :HY] * flip(from_xhi[...])
-    side[p] = side[p] * flip(jnp.where(lane_of(BX) < HZ, from_yhi[...], from_ylo[...]))
-    column[p] = column[p] * flip(jnp.where(z_parts(p), from_zlo[...], from_zhi[...]))
-
-
-def rates(act, spin, side, column, odds, gain, h, a, v, xlo, xhi, ylo, yhi, zed, sent):
+    low_x, high_x, y_side, z_side = halo
+    spin[p, 0, :HY] = spin[p, 0, :HY] * flip(low_x)
+    spin[p, BX + 1, :HY] = spin[p, BX + 1, :HY] * flip(high_x)
+    side[p] = side[p] * flip(y_side)
+    column[p] = column[p] * flip(z_side)
+
+
+def rates(act, where, spin, side, column, odds, gain, h, a, v, x_one, x_two, y_one, y_two, zed, sent):
     p = 1 - act
     lane = lane_of()
     one_row = lane_of(1)
@@ -200,12 +207,11 @@
             x = i * UNROLL + j
             odd = odd_row(j + act)
             here = spin[p, x + 1, :HY]
-            turned = jnp.where(odd, roll(here, -1), roll(here, 1))
-            edge = jnp.where(odd, pltpu.roll(ends, (HZ - 1 - x) % BZ, 1), pltpu.roll(ends, (BZ - x) % BZ, 1))
-            at_edge = lane % HZ == jnp.where(odd, HZ - 1, 0)
+            joined = jnp.where(lane % HZ == jnp.where(odd, 0, HZ - 1), pltpu.roll(ends, (BZ + HZ - 2 * x) % BZ, 1), here)
+            turned = jnp.where(odd, roll(joined, -1), roll(joined, 1))
             beside = spin[p, x, :HY] + spin[p, x + 2, :HY]
             beside = beside + jnp.where(top, spin[p, x + 1, HY + 1 : HY + 2], pltpu.roll(here, 1, 0)) + spin[p, x + 1, 1 : HY + 1]
-            beside = beside + here + jnp.where(at_edge, edge, turned)
+            beside = beside + here + turned
             g = h[act, x] - 0.5 * beside
             gain[x] = g
             grown = 1.0 + jnp.exp(2.0 * spin[act, x + 1, :HY] * g)
@@ -213,30 +219,26 @@
             root = v[x] * grown
             square = root * root
             odds[x] = square
-            marked = jnp.where(odd, roll(square, HZ + 1), square)
-            packed = jnp.where(lane % HZ == x, pltpu.roll(marked, x, 1), packed)
+            packed = add_face(packed, square, x, odd)
         return packed, summed
 
     packed, summed = lax.fori_loop(0, BX // UNROLL, step, (jnp.zeros((HY, BZ), F32), jnp.zeros((HY, BZ), F32)))
-    xlo[...] = odds[0]
-    xhi[...] = odds[BX - 1]
-    for x in range(BX):
-        ylo[x : x + 1] = odds[x, :1]
-        yhi[x : x + 1] = odds[x, HY - 1 :]
+    x_one[...], x_two[...] = sort_faces(where[1], odds[0], odds[BX - 1])
+    for x in range(BX):
+        y_one[x : x + 1], y_two[x : x + 1] = sort_faces(where[2], odds[x, :1], odds[x, HY - 1 :])
     zed[...] = packed
     sent[...] = jnp.broadcast_to(jnp.sum(summed, axis=0, keepdims=True), sent.shape)
 
 
 def first_kernel(
-    from_xlo, from_xhi, from_ylo, from_yhi, from_zlo, from_zhi, h, a, v, v_hbm, spin_in,
-    spin, side, column, energy, fields, clock, odds, gain, xlo, xhi, ylo, yhi, zed, sent, v_next, arrived,
+    where, from_x_one, from_x_two, from_y_one, from_y_two, from_z_one, from_z_two, h, a, v, v_hbm, spin_in,
+    spin, side, column, energy, fields, clock, odds, gain, x_one, x_two, y_one, y_two, zed, sent, v_next, arrived,
 ):
     copies = fetch([(v_hbm.at[1], v_next)], arrived)
     for p in range(2):
-        spin[p, 0, :HY] = from_xlo[p]
-        spin[p, BX + 1, :HY] = from_xhi[p]
-        side[p] = jnp.where(lane_of(BX) < HZ, from_yhi[p], from_ylo[p])
-        column[p] = jnp.where(z_parts(p), from_zlo[p], from_zhi[p])
+        spin[p, 0, :HY], spin[p, BX + 1, :HY], side[p], column[p] = halo_parts(
+            where, from_x_one[p], from_x_two[p], from_y_one[p], from_y_two[p], from_z_one[p], from_z_two[p]
+        )
     of_field = jnp.zeros((HY, BZ), F32)
     for x in range(BX):
         of_field = of_field + spin[1, x + 1, :HY] * h[1, x]
@@ -244,20 +246,22 @@
     fields[1] = eighth(of_field)
     energy[...] = jnp.zeros(energy.shape, F32)
     clock[...] = jnp.zeros(clock.shape, F32)
-    rates(0, spin, side, column, odds, gain, h, a, v, xlo, xhi, ylo, yhi, zed, sent)
+    rates(0, where, spin, side, column, odds, gain, h, a, v, x_one, x_two, y_one, y_two, zed, sent)
     copies[0].wait()
 
 
 def section_kernel(
-    act, half, where, gathered, from_xlo, from_xhi, from_ylo, from_yhi, from_zlo, from_zhi, h, a, v, v_hbm,
+    act, half, where, gathered, from_x_one, from_x_two, from_y_one, from_y_two, from_z_one, from_z_two, h, a, v, v_hbm,
     spin_in, side_in, column_in, energy_in, fields_in, clock_in, odds_in, gain_in,
-    spin, side, column, energy, fields, clock, odds, gain, xlo, xhi, ylo, yhi, zed, sent, v_next, arrived,
+    spin, side, column, energy, fields, clock, odds, gain, x_one, x_two, y_one, y_two, zed, sent, v_next, arrived,
 ):
     k = where[0]
     copies = fetch([(v_hbm.at[jnp.minimum(k + 1, SECTIONS - 1)], v_next)], arrived)
-    halo = (from_xlo, from_xhi, from_ylo, from_yhi, from_zlo, from_zhi)
+    halo = halo_parts(
+        where, from_x_one[...], from_x_two[...], from_y_one[...], from_y_two[...], from_z_one[...], from_z_two[...]
+    )
     advance(k, 1 - act, half, gathered, halo, spin, side, column, odds, gain, h, energy, fields, clock)
-    rates(act, spin, side, column, odds, gain, h, a, v, xlo, xhi, ylo, yhi, zed, sent)
+    rates(act, where, spin, side, column, odds, gain, h, a, v, x_one, x_two, y_one, y_two, zed, sent)
     copies[0].wait()
 
 
@@ -299,7 +303,7 @@
     return pl.pallas_call(
         kernel,
         out_shape=[pltpu.HBM(shape, F32) if i in far_out else jax.ShapeDtypeStruct(shape, F32) for i, shape in enumerate(outputs)],
-        in_specs=[away if i in far else scalar if x.shape == (1,) else held for i, x in enumerate(inputs)],
+        in_specs=[away if i in far else scalar if x.shape == (4,) else held for i, x in enumerate(inputs)],
         out_specs=[away if i in far_out else held for i in range(len(outputs))],
         input_output_aliases=aliases or {},
         scratch_shapes=scratch,
@@ -308,13 +312,13 @@
     )(*inputs)
 
 
-def swap(xlo, xhi, ylo, yhi, zlo, zhi):
+def swap(x_one, x_two, y_one, y_two, z_one, z_two):
     got = []
-    for axis, low, high in (("gx", xlo, xhi), ("gy", ylo, yhi), ("gz", zlo, zhi)):
+    for axis, one, two in (("gx", x_one, x_two), ("gy", y_one, y_two), ("gz", z_one, z_two)):
         count = lax.axis_size(axis)
-        up = [(i, (i + 1) % count) for i in range(count)]
-        got.append(lax.ppermute(high, axis, up))
-        got.append(lax.ppermute(low, axis, [(b, a) for a, b in up]))
+        for block, shift in ((one, 0), (two, 1)):
+            pairs = [(i, (i + (1 if i % 2 == shift else -1)) % count) for i in range(count)]
+            got.append(lax.ppermute(block, axis, pairs))
     return got
 
 
@@ -333,9 +337,14 @@
     state = [spin_shape, (2, BX, BZ), (2, *tile), (SECTIONS, 8, BZ), (2, 8, BZ), (8, BZ), block, block]
     sent_shape = (devices, BZ)
     dma = pltpu.SemaphoreType.DMA
+    evens = [1 - lax.axis_index(axis) % 2 for axis in AXES]
+
+    def where(k):
+        return jnp.stack([jnp.asarray(k, jnp.int32), *evens]).astype(jnp.int32)
+
     streams = [dma((1,))]
     spin, *sides = call(
-        spins_kernel, (occupancy,), [spin_shape] + [(2, *face) for face in faces], far=(0,),
+        spins_kernel, (where(0), occupancy), [spin_shape] + [(2, *face) for face in faces], far=(1,),
         scratch=[pltpu.VMEM((BX, BY, BZ), jnp.int32), dma((BX // CHUNK,))],
     )
     halo = swap(*sides, sides[-1])
@@ -349,16 +358,16 @@
         ],
     )
     carried = call(
-        first_kernel, (*halo, h, a, v, draws, spin), state + faces + [sent_shape, block], {10: 0}, far=(9,), scratch=streams,
+        first_kernel, (where(0), *halo, h, a, v, draws, spin), state + faces + [sent_shape, block], {11: 0}, far=(10,), scratch=streams,
     )
 
     def section(k, act, carried):
-        *kept, xlo, xhi, ylo, yhi, zed, sent, v = carried
+        *kept, x_one, x_two, y_one, y_two, zed, sent, v = carried
         gathered = spread(sent)
-        halo = swap(xlo, xhi, ylo, yhi, zed, zed)
+        halo = swap(x_one, x_two, y_one, y_two, zed, zed)
         return call(
             functools.partial(section_kernel, act, half),
-            (jnp.full((1,), k, jnp.int32), gathered, *halo, h, a, v, draws, *kept), state + faces + [sent_shape, block],
+            (where(k), gathered, *halo, h, a, v, draws, *kept), state + faces + [sent_shape, block],
             {12 + i: i for i in range(len(state))}, far=(11,), scratch=streams,
         )
 

time: 250 us -> 244 us (0.976)
  waiting for transfers between devices: 36.2 us -> 28.8 us
  blocking collectives: 26.4 us -> 22.1 us
  Pallas kernels: 31.3 us -> 35.3 us
    all_to_all x8, waiting for transfers between devices: 21.5 us -> 9.99 us  [spread(): return lax.all_to_all(sent, AXES, 0, 0, tiled=True)]
    ppermute x48, starting transfers between devices: 70.4 us -> 79.8 us  [swap(): got.append(lax.ppermute(block, axis, pairs))]
    all_to_all x8, starting transfers between devices: 82.4 us -> 73.6 us  [spread(): return lax.all_to_all(sent, AXES, 0, 0, tiled=True)]
    all_to_all x1, blocking collectives: 26.4 us -> 22.1 us  [spread(): return lax.all_to_all(sent, AXES, 0, 0, tiled=True)]
    ppermute x48, waiting for transfers between devices: 14.7 us -> 18.8 us  [swap(): got.append(lax.ppermute(block, axis, pairs))]
    pallas_call x13, Pallas kernels: 31.3 us -> 35.3 us  [call(): pl.pallas_call(kernel, out_shape=[pltpu.HBM(shape, F32) if i in far_out e...]
  transfers between devices with their start and end apart: 56 -> 56, of which waited for: 18 -> 8; matrix products, arithmetic and copies ran while one was open for 0% -> 0% of each run, Pallas kernels for 4% -> 4%
where the time goes in v1:
time: 244 us; the launch traced here: 241 us
  starting transfers between devices  153 us (63%)
  Pallas kernels  35.3 us (14%)
  waiting for transfers between devices  28.8 us (12%)
  blocking collectives  22.1 us (9%)
    ppermute x48, starting transfers between devices, swap(): got.append(lax.ppermute(block, axis, pairs))  79.8 us
    all_to_all x8, starting transfers between devices, spread(): return lax.all_to_all(sent, AXES, 0, 0, tiled=True)  73.6 us
    pallas_call x13, Pallas kernels, call(): pl.pallas_call(kernel, out_shape=[pltpu.HBM(shape, F32) if i in far_out e...  35.3 us
    all_to_all x1, blocking collectives, spread(): return lax.all_to_all(sent, AXES, 0, 0, tiled=True)  22.1 us
    ppermute x48, waiting for transfers between devices, swap(): got.append(lax.ppermute(block, axis, pairs))  18.8 us
    all_to_all x8, waiting for transfers between devices, spread(): return lax.all_to_all(sent, AXES, 0, 0, tiled=True)  9.99 us
  transfers between devices with their start and end apart: 56, of which 8 were waited for; matrix products, arithmetic and copies ran while one was open for 0% of the time, Pallas kernels for 4%

profile of v1, /device:TPU:32, one launch (start us, length us, event | category | flops | bytes accessed | tf_op | source)
XLA Modules:
  0.0 241.3 jit_solution(8445156480017331378)
XLA Ops:
  0.7 2.7 %shard_map.59 = (f32[2,18,40,128]{3,2,1,0:T(8,128)S(1)}, f32[2,32,128]{2,1,0:T(8,128)S(1)}, f32[2,32,128]{2,1,0:T(8,128)S(1)}, f32[2,16,128]{2,1,0:T(8,128)S(1)}...) custom-call(s32[4]{0:T(128)S(1)} %add_add_fusion.3.where, s32[16,64,128]{2,1,0:T(8,128)} %occ_hbm.1), custom_call_target="tpu_custom_call" | custom-call | flops 1000000 | bytes 1000000 | tf_op jit(solution)/shard_map/pallas_call | solution.py:303
  3.6 1.6 collective-permute-start.12
  5.2 3.0 %collective-permute-start.13 = (f32[2,32,128]{2,1,0:T(8,128)S(1)}, f32[2,32,128]{2,1,0:T(8,128)S(1)}, u32[]{:S(2)}, u32[]{:S(2)}) collective-permute-start(f32[2,32,128]{2,1,0:T(8,128)S(1)} %get-tuple-element.428), channel_id=1, source_target_pairs={{0,224},{32,64},{64,32},{96,128},{128,96},{160,192},{192,160},{224... | collective-permute-start | bytes 98312 | tf_op jit(solution)/shard_map/ppermute | solution.py:321
  8.3 3.7 %collective-permute-start.17 = (f32[2,32,128]{2,1,0:T(8,128)S(1)}, f32[2,32,128]{2,1,0:T(8,128)S(1)}, u32[]{:S(2)}, u32[]{:S(2)}) collective-permute-start(f32[2,32,128]{2,1,0:T(8,128)S(1)} %get-tuple-element.431), channel_id=1, source_target_pairs={{0,7},{1,2},{2,1},{3,4},{4,3},{5,6},{6,5},{7,0},{8,15},{9,10},{10,... | collective-permute-start | bytes 98312 | tf_op jit(solution)/shard_map/ppermute | solution.py:321
  12.0 1.9 collective-permute-start.15
  13.9 7.3 %shard_map.60 = (f32[2,16,32,128]{3,2,1,0:T(8,128)S(1)}, f32[2,16,32,128]{3,2,1,0:T(8,128)S(1)}, f32[16,32,128]{2,1,0:T(8,128)S(1)}, f32[8,16,32,128]{3,2,1,0:T(8,128)}) custom-call(f32[16,64,128]{2,1,0:T(8,128)} %field_hbm.1, f32[16,64,128]{2,1,0:T(8,128)} %attempt_hbm.1, f32[8,16,64,64]{3,2,1,0:T(8,128)} %uniforms.1), custom_call_target="tpu_custom_call" | custom-call | flops 1000000 | bytes 1000000 | tf_op jit(solution)/shard_map/pallas_call | solution.py:303
  21.2 2.4 shard_map.61
  23.6 150.0 %while.41 = (s32[]{:T(128)}, f32[2,18,40,128]{3,2,1,0:T(8,128)S(1)}, f32[2,16,128]{2,1,0:T(8,128)S(1)}, f32[2,32,128]{2,1,0:T(8,128)S(1)}, f32[8,8,128]{2,1,0:T(...) while((s32[]{:T(128)}, ...), condition=%wide.region_1.2_spmd, body=%wide.region_0.1_spmd.sunk | while | flops 2000029 | bytes 3442649 | solution.py:377
  23.7 9.4 %all-to-all-start = ((f32[256,1,128]{2,1,0:T(1,128)}), f32[256,1,128]{2,1,0:T(1,128)S(1)}, u32[]{:S(2)}, u32[]{:S(2)}) async-start(f32[256,1,128]{2,1,0:T(1,128)} %bitcast.38), calls=%async_computation | async-start | bytes 262144 | tf_op jit(solution)/shard_map/while/body/eval_jaxpr/all_to_all | solution.py:326
  33.2 2.0 collective-permute-start.4
  35.2 1.5 collective-permute-start.5
  36.7 1.5 collective-permute-start
  38.2 2.9 %collective-permute-start.1 = (f32[32,128]{1,0:T(8,128)S(1)}, f32[32,128]{1,0:T(8,128)S(1)}, u32[]{:S(2)}, u32[]{:S(2)}) collective-permute-start(f32[32,128]{1,0:T(8,128)S(1)} %get-tuple-element.748), channel_id=1, source_target_pairs={{0,224},{32,64},{64,32},{96,128},{128,96},{160,192},{192,160},{224... | collective-permute-start | bytes 49160 | tf_op jit(solution)/shard_map/while/body/eval_jaxpr/ppermute | solution.py:321
  41.0 1.9 collective-permute-start.3
  43.0 2.7 %collective-permute-done.3.from_y_two = f32[16,128]{1,0:T(8,128)S(1)} collective-permute-done((f32[16,128]{1,0:T(8,128)S(1)}, f32[16,128]{1,0:T(8,128)S(1)}, u32[]{:S(2)}, u32[]{:S(2)}) %collective-permute-start.3) | collective-permute-done | bytes 8224 | tf_op jit(solution)/shard_map/while/body/eval_jaxpr/ppermute | solution.py:321
  45.7 2.7 %eval_jaxpr.10 = (f32[2,18,40,128]{3,2,1,0:T(8,128)S(1)}, f32[2,16,128]{2,1,0:T(8,128)S(1)}, f32[2,32,128]{2,1,0:T(8,128)S(1)}, f32[8,8,128]{2,1,0:T(8,128)S(1)}...) custom-call(s32[4]{0:T(128)S(1)} %add_add_fusion.7.where, ...), custom_call_target="tpu_custom_call", output_to_operand_aliasing={{0}: (12, {}), {1}: (13, {}), {2}: (14, {}), {3}: (15, {}),... | custom-call | flops 1000000 | bytes 1000000 | tf_op jit(solution)/shard_map/while/body/eval_jaxpr/pallas_call | solution.py:303
  48.4 9.7 %all-to-all-start.1 = ((f32[256,1,128]{2,1,0:T(1,128)}), f32[256,1,128]{2,1,0:T(1,128)S(1)}, u32[]{:S(2)}, u32[]{:S(2)}) async-start(f32[256,1,128]{2,1,0:T(1,128)} %bitcast.40), calls=%async_computation.1 | async-start | bytes 262144 | tf_op jit(solution)/shard_map/while/body/eval_jaxpr/all_to_all | solution.py:326
  58.3 2.0 collective-permute-start.10
  61.7 1.5 collective-permute-start.6
  63.2 2.9 %collective-permute-start.7 = (f32[32,128]{1,0:T(8,128)S(1)}, f32[32,128]{1,0:T(8,128)S(1)}, u32[]{:S(2)}, u32[]{:S(2)}) collective-permute-start(f32[32,128]{1,0:T(8,128)S(1)} %get-tuple-element.686), channel_id=1, source_target_pairs={{0,224},{32,64},{64,32},{96,128},{128,96},{160,192},{192,160},{224... | collective-permute-start | bytes 49160 | tf_op jit(solution)/shard_map/while/body/eval_jaxpr/ppermute | solution.py:321
  66.1 1.9 collective-permute-start.9
  68.0 2.7 %collective-permute-done.9.from_y_two = f32[16,128]{1,0:T(8,128)S(1)} collective-permute-done((f32[16,128]{1,0:T(8,128)S(1)}, f32[16,128]{1,0:T(8,128)S(1)}, u32[]{:S(2)}, u32[]{:S(2)}) %collective-permute-start.9) | collective-permute-done | bytes 8224 | tf_op jit(solution)/shard_map/while/body/eval_jaxpr/ppermute | solution.py:321
  70.7 2.7 %eval_jaxpr.11 = (f32[2,18,40,128]{3,2,1,0:T(8,128)S(1)}, f32[2,16,128]{2,1,0:T(8,128)S(1)}, f32[2,32,128]{2,1,0:T(8,128)S(1)}, f32[8,8,128]{2,1,0:T(8,128)S(1)}...) custom-call(s32[4]{0:T(128)S(1)} %add_add_fusion.6.where, ...), custom_call_target="tpu_custom_call", output_to_operand_aliasing={{0}: (12, {}), {1}: (13, {}), {2}: (14, {}), {3}: (15, {}),... | custom-call | flops 1000000 | bytes 1000000 | tf_op jit(solution)/shard_map/while/body/eval_jaxpr/pallas_call | solution.py:303
  73.4 9.7 %all-to-all-start = ((f32[256,1,128]{2,1,0:T(1,128)}), f32[256,1,128]{2,1,0:T(1,128)S(1)}, u32[]{:S(2)}, u32[]{:S(2)}) async-start(f32[256,1,128]{2,1,0:T(1,128)} %bitcast.38), calls=%async_computation | async-start | bytes 262144 | tf_op jit(solution)/shard_map/while/body/eval_jaxpr/all_to_all | solution.py:326
  83.3 2.0 collective-permute-start.4
  85.3 1.5 collective-permute-start.5
  86.8 1.5 collective-permute-start
  88.3 2.9 %collective-permute-start.1 = (f32[32,128]{1,0:T(8,128)S(1)}, f32[32,128]{1,0:T(8,128)S(1)}, u32[]{:S(2)}, u32[]{:S(2)}) collective-permute-start(f32[32,128]{1,0:T(8,128)S(1)} %get-tuple-element.748), channel_id=1, source_target_pairs={{0,224},{32,64},{64,32},{96,128},{128,96},{160,192},{192,160},{224... | collective-permute-start | bytes 49160 | tf_op jit(solution)/shard_map/while/body/eval_jaxpr/ppermute | solution.py:321
  91.2 1.9 collective-permute-start.3
  93.1 2.7 %collective-permute-done.3.from_y_two = f32[16,128]{1,0:T(8,128)S(1)} collective-permute-done((f32[16,128]{1,0:T(8,128)S(1)}, f32[16,128]{1,0:T(8,128)S(1)}, u32[]{:S(2)}, u32[]{:S(2)}) %collective-permute-start.3) | collective-permute-done | bytes 8224 | tf_op jit(solution)/shard_map/while/body/eval_jaxpr/ppermute | solution.py:321
  95.8 2.7 %eval_jaxpr.10 = (f32[2,18,40,128]{3,2,1,0:T(8,128)S(1)}, f32[2,16,128]{2,1,0:T(8,128)S(1)}, f32[2,32,128]{2,1,0:T(8,128)S(1)}, f32[8,8,128]{2,1,0:T(8,128)S(1)}...) custom-call(s32[4]{0:T(128)S(1)} %add_add_fusion.7.where, ...), custom_call_target="tpu_custom_call", output_to_operand_aliasing={{0}: (12, {}), {1}: (13, {}), {2}: (14, {}), {3}: (15, {}),... | custom-call | flops 1000000 | bytes 1000000 | tf_op jit(solution)/shard_map/while/body/eval_jaxpr/pallas_call | solution.py:303
  98.5 9.7 %all-to-all-start.1 = ((f32[256,1,128]{2,1,0:T(1,128)}), f32[256,1,128]{2,1,0:T(1,128)S(1)}, u32[]{:S(2)}, u32[]{:S(2)}) async-start(f32[256,1,128]{2,1,0:T(1,128)} %bitcast.40), calls=%async_computation.1 | async-start | bytes 262144 | tf_op jit(solution)/shard_map/while/body/eval_jaxpr/all_to_all | solution.py:326
  108.4 2.0 collective-permute-start.10
  111.9 1.5 collective-permute-start.6
  113.3 2.9 %collective-permute-start.7 = (f32[32,128]{1,0:T(8,128)S(1)}, f32[32,128]{1,0:T(8,128)S(1)}, u32[]{:S(2)}, u32[]{:S(2)}) collective-permute-start(f32[32,128]{1,0:T(8,128)S(1)} %get-tuple-element.686), channel_id=1, source_target_pairs={{0,224},{32,64},{64,32},{96,128},{128,96},{160,192},{192,160},{224... | collective-permute-start | bytes 49160 | tf_op jit(solution)/shard_map/while/body/eval_jaxpr/ppermute | solution.py:321
  116.2 1.9 collective-permute-start.9
  118.1 2.7 %collective-permute-done.9.from_y_two = f32[16,128]{1,0:T(8,128)S(1)} collective-permute-done((f32[16,128]{1,0:T(8,128)S(1)}, f32[16,128]{1,0:T(8,128)S(1)}, u32[]{:S(2)}, u32[]{:S(2)}) %collective-permute-start.9) | collective-permute-done | bytes 8224 | tf_op jit(solution)/shard_map/while/body/eval_jaxpr/ppermute | solution.py:321
  120.9 2.7 %eval_jaxpr.11 = (f32[2,18,40,128]{3,2,1,0:T(8,128)S(1)}, f32[2,16,128]{2,1,0:T(8,128)S(1)}, f32[2,32,128]{2,1,0:T(8,128)S(1)}, f32[8,8,128]{2,1,0:T(8,128)S(1)}...) custom-call(s32[4]{0:T(128)S(1)} %add_add_fusion.6.where, ...), custom_call_target="tpu_custom_call", output_to_operand_aliasing={{0}: (12, {}), {1}: (13, {}), {2}: (14, {}), {3}: (15, {}),... | custom-call | flops 1000000 | bytes 1000000 | tf_op jit(solution)/shard_map/while/body/eval_jaxpr/pallas_call | solution.py:303
  123.5 9.7 %all-to-all-start = ((f32[256,1,128]{2,1,0:T(1,128)}), f32[256,1,128]{2,1,0:T(1,128)S(1)}, u32[]{:S(2)}, u32[]{:S(2)}) async-start(f32[256,1,128]{2,1,0:T(1,128)} %bitcast.38), calls=%async_computation | async-start | bytes 262144 | tf_op jit(solution)/shard_map/while/body/eval_jaxpr/all_to_all | solution.py:326
  133.5 2.0 collective-permute-start.4
  135.5 1.5 collective-permute-start.5
  136.9 1.5 collective-permute-start
  138.4 2.9 %collective-permute-start.1 = (f32[32,128]{1,0:T(8,128)S(1)}, f32[32,128]{1,0:T(8,128)S(1)}, u32[]{:S(2)}, u32[]{:S(2)}) collective-permute-start(f32[32,128]{1,0:T(8,128)S(1)} %get-tuple-element.748), channel_id=1, source_target_pairs={{0,224},{32,64},{64,32},{96,128},{128,96},{160,192},{192,160},{224... | collective-permute-start | bytes 49160 | tf_op jit(solution)/shard_map/while/body/eval_jaxpr/ppermute | solution.py:321
  141.3 1.9 collective-permute-start.3
  143.2 2.7 %collective-permute-done.3.from_y_two = f32[16,128]{1,0:T(8,128)S(1)} collective-permute-done((f32[16,128]{1,0:T(8,128)S(1)}, f32[16,128]{1,0:T(8,128)S(1)}, u32[]{:S(2)}, u32[]{:S(2)}) %collective-permute-start.3) | collective-permute-done | bytes 8224 | tf_op jit(solution)/shard_map/while/body/eval_jaxpr/ppermute | solution.py:321
  145.9 2.7 %eval_jaxpr.10 = (f32[2,18,40,128]{3,2,1,0:T(8,128)S(1)}, f32[2,16,128]{2,1,0:T(8,128)S(1)}, f32[2,32,128]{2,1,0:T(8,128)S(1)}, f32[8,8,128]{2,1,0:T(8,128)S(1)}...) custom-call(s32[4]{0:T(128)S(1)} %add_add_fusion.7.where, ...), custom_call_target="tpu_custom_call", output_to_operand_aliasing={{0}: (12, {}), {1}: (13, {}), {2}: (14, {}), {3}: (15, {}),... | custom-call | flops 1000000 | bytes 1000000 | tf_op jit(solution)/shard_map/while/body/eval_jaxpr/pallas_call | solution.py:303
  148.6 9.7 %all-to-all-start.1 = ((f32[256,1,128]{2,1,0:T(1,128)}), f32[256,1,128]{2,1,0:T(1,128)S(1)}, u32[]{:S(2)}, u32[]{:S(2)}) async-start(f32[256,1,128]{2,1,0:T(1,128)} %bitcast.40), calls=%async_computation.1 | async-start | bytes 262144 | tf_op jit(solution)/shard_map/while/body/eval_jaxpr/all_to_all | solution.py:326
  158.5 2.0 collective-permute-start.10
  162.0 1.5 collective-permute-start.6
  163.4 2.9 %collective-permute-start.7 = (f32[32,128]{1,0:T(8,128)S(1)}, f32[32,128]{1,0:T(8,128)S(1)}, u32[]{:S(2)}, u32[]{:S(2)}) collective-permute-start(f32[32,128]{1,0:T(8,128)S(1)} %get-tuple-element.686), channel_id=1, source_target_pairs={{0,224},{32,64},{64,32},{96,128},{128,96},{160,192},{192,160},{224... | collective-permute-start | bytes 49160 | tf_op jit(solution)/shard_map/while/body/eval_jaxpr/ppermute | solution.py:321
  166.3 1.9 collective-permute-start.9
  168.3 2.7 %collective-permute-done.9.from_y_two = f32[16,128]{1,0:T(8,128)S(1)} collective-permute-done((f32[16,128]{1,0:T(8,128)S(1)}, f32[16,128]{1,0:T(8,128)S(1)}, u32[]{:S(2)}, u32[]{:S(2)}) %collective-permute-start.9) | collective-permute-done | bytes 8224 | tf_op jit(solution)/shard_map/while/body/eval_jaxpr/ppermute | solution.py:321
  171.0 2.7 %eval_jaxpr.11 = (f32[2,18,40,128]{3,2,1,0:T(8,128)S(1)}, f32[2,16,128]{2,1,0:T(8,128)S(1)}, f32[2,32,128]{2,1,0:T(8,128)S(1)}, f32[8,8,128]{2,1,0:T(8,128)S(1)}...) custom-call(s32[4]{0:T(128)S(1)} %add_add_fusion.6.where, ...), custom_call_target="tpu_custom_call", output_to_operand_aliasing={{0}: (12, {}), {1}: (13, {}), {2}: (14, {}), {3}: (15, {}),... | custom-call | flops 1000000 | bytes 1000000 | tf_op jit(solution)/shard_map/while/body/eval_jaxpr/pallas_call | solution.py:303
  173.7 9.7 %all-to-all-start.2 = ((f32[256,1,128]{2,1,0:T(1,128)}), f32[256,1,128]{2,1,0:T(1,128)S(1)}, u32[]{:S(2)}, u32[]{:S(2)}) async-start(f32[256,1,128]{2,1,0:T(1,128)} %bitcast.14), calls=%async_computation.2 | async-start | bytes 262144 | tf_op jit(solution)/shard_map/all_to_all | solution.py:326
  183.8 2.0 collective-permute-start.22
  187.2 1.5 collective-permute-start.18
  188.7 2.9 %collective-permute-start.19 = (f32[32,128]{1,0:T(8,128)S(1)}, f32[32,128]{1,0:T(8,128)S(1)}, u32[]{:S(2)}, u32[]{:S(2)}) collective-permute-start(f32[32,128]{1,0:T(8,128)S(1)} %get-tuple-element.454), channel_id=1, source_target_pairs={{0,224},{32,64},{64,32},{96,128},{128,96},{160,192},{192,160},{224... | collective-permute-start | bytes 49160 | tf_op jit(solution)/shard_map/ppermute | solution.py:321
  191.6 1.9 collective-permute-start.21
  193.5 2.7 %collective-permute-done.21.from_y_two = f32[16,128]{1,0:T(8,128)S(1)} collective-permute-done((f32[16,128]{1,0:T(8,128)S(1)}, f32[16,128]{1,0:T(8,128)S(1)}, u32[]{:S(2)}, u32[]{:S(2)}) %collective-permute-start.21) | collective-permute-done | bytes 8224 | tf_op jit(solution)/shard_map/ppermute | solution.py:321
  196.2 2.7 %shard_map.62 = (f32[2,18,40,128]{3,2,1,0:T(8,128)S(1)}, f32[2,16,128]{2,1,0:T(8,128)S(1)}, f32[2,32,128]{2,1,0:T(8,128)S(1)}, f32[8,8,128]{2,1,0:T(8,128)S(1)},...) custom-call(s32[4]{0:T(128)S(1)} %add_add_fusion.2.where, ...), custom_call_target="tpu_custom_call", output_to_operand_aliasing={{0}: (12, {}), {1}: (13, {}), {2}: (14, {}), {3}: (15, {}),... | custom-call | flops 1000000 | bytes 1000000 | tf_op jit(solution)/shard_map/pallas_call | solution.py:303
  199.0 22.1 %all_to_all.53 = f32[256,1,128]{2,1,0:T(1,128)S(1)} all-to-all(f32[256,1,128]{2,1,0:T(1,128)S(1)} %bitcast.47), channel_id=1, replica_groups=mesh['gx'=8,'gy'=4,'gz'=8] {'gx','gy','gz'}, dimensions={0} | all-to-all | bytes 262144 | tf_op jit(solution)/shard_map/all_to_all | solution.py:326
  222.1 6.1 %all-to-all-start.4 = ((f32[256,1,128]{2,1,0:T(1,128)}), f32[256,1,128]{2,1,0:T(1,128)S(1)}, u32[]{:S(2)}, u32[]{:S(2)}) async-start(f32[256,1,128]{2,1,0:T(1,128)} %bitcast.20), calls=%async_computation.4 | async-start | bytes 262144 | tf_op jit(solution)/shard_map/all_to_all | solution.py:326
  228.2 2.6 %shard_map.64 = f32[16,64,128]{2,1,0:T(8,128)} custom-call(f32[2,18,40,128]{3,2,1,0:T(8,128)S(1)} %get-tuple-element.474.spin), custom_call_target="tpu_custom_call" | custom-call | flops 1000000 | bytes 1000000 | tf_op jit(solution)/shard_map/pallas_call | solution.py:303
  230.8 10.0 %all-to-all-done.4 = f32[256,1,128]{2,1,0:T(1,128)S(1)} async-done(((f32[256,1,128]{2,1,0:T(1,128)}), f32[256,1,128]{2,1,0:T(1,128)S(1)}, u32[]{:S(2)}, u32[]{:S(2)}) %all-to-all-start.4) | async-done | bytes 131104 | tf_op jit(solution)/shard_map/all_to_all | solution.py:326
  (71 shorter events, 10.1 us)
Async XLA Ops:
  3.5 8.5 %collective-permute-start.14 = (f32[2,16,128]{2,1,0:T(8,128)S(1)}, f32[2,16,128]{2,1,0:T(8,128)S(1)}, u32[]{:S(2)}, u32[]{:S(2)}) collective-permute-start(f32[2,16,128]{2,1,0:T(8,128)S(1)} %get-tuple-element.429), channel_id=1, source_target_pairs={{0,8},{8,0},{16,24},{24,16},{1,9},{9,1},{17,25},{25,17},{2,10},{10... | collective-permute-start | bytes 49160 | tf_op jit(solution)/shard_map/ppermute | solution.py:321
  3.6 17.6 %collective-permute-start.12 = (f32[2,32,128]{2,1,0:T(8,128)S(1)}, f32[2,32,128]{2,1,0:T(8,128)S(1)}, u32[]{:S(2)}, u32[]{:S(2)}) collective-permute-start(f32[2,32,128]{2,1,0:T(8,128)S(1)} %get-tuple-element.427), channel_id=1, source_target_pairs={{0,32},{32,0},{64,96},{96,64},{128,160},{160,128},{192,224},{224,1... | collective-permute-start | bytes 98312 | tf_op jit(solution)/shard_map/ppermute | solution.py:321
  5.2 16.0 %collective-permute-start.13 = (f32[2,32,128]{2,1,0:T(8,128)S(1)}, f32[2,32,128]{2,1,0:T(8,128)S(1)}, u32[]{:S(2)}, u32[]{:S(2)}) collective-permute-start(f32[2,32,128]{2,1,0:T(8,128)S(1)} %get-tuple-element.428), channel_id=1, source_target_pairs={{0,224},{32,64},{64,32},{96,128},{128,96},{160,192},{192,160},{224... | collective-permute-start | bytes 98312 | tf_op jit(solution)/shard_map/ppermute | solution.py:321
  8.2 13.1 %collective-permute-start.16 = (f32[2,32,128]{2,1,0:T(8,128)S(1)}, f32[2,32,128]{2,1,0:T(8,128)S(1)}, u32[]{:S(2)}, u32[]{:S(2)}) collective-permute-start(f32[2,32,128]{2,1,0:T(8,128)S(1)} %get-tuple-element.431), channel_id=1, source_target_pairs={{0,1},{1,0},{2,3},{3,2},{4,5},{5,4},{6,7},{7,6},{8,9},{9,8},{10,11... | collective-permute-start | bytes 98312 | tf_op jit(solution)/shard_map/ppermute | solution.py:321
  8.3 13.0 %collective-permute-start.17 = (f32[2,32,128]{2,1,0:T(8,128)S(1)}, f32[2,32,128]{2,1,0:T(8,128)S(1)}, u32[]{:S(2)}, u32[]{:S(2)}) collective-permute-start(f32[2,32,128]{2,1,0:T(8,128)S(1)} %get-tuple-element.431), channel_id=1, source_target_pairs={{0,7},{1,2},{2,1},{3,4},{4,3},{5,6},{6,5},{7,0},{8,15},{9,10},{10,... | collective-permute-start | bytes 98312 | tf_op jit(solution)/shard_map/ppermute | solution.py:321
  12.0 9.2 %collective-permute-start.15 = (f32[2,16,128]{2,1,0:T(8,128)S(1)}, f32[2,16,128]{2,1,0:T(8,128)S(1)}, u32[]{:S(2)}, u32[]{:S(2)}) collective-permute-start(f32[2,16,128]{2,1,0:T(8,128)S(1)} %get-tuple-element.430), channel_id=1, source_target_pairs={{0,24},{8,16},{16,8},{24,0},{1,25},{9,17},{17,9},{25,1},{2,26},{10... | collective-permute-start | bytes 49160 | tf_op jit(solution)/shard_map/ppermute | solution.py:321
  23.7 22.0 %all-to-all-start = ((f32[256,1,128]{2,1,0:T(1,128)}), f32[256,1,128]{2,1,0:T(1,128)S(1)}, u32[]{:S(2)}, u32[]{:S(2)}) async-start(f32[256,1,128]{2,1,0:T(1,128)} %bitcast.38), calls=%async_computation | async-start | bytes 262144 | tf_op jit(solution)/shard_map/while/body/eval_jaxpr/all_to_all | solution.py:326
  33.0 8.0 %collective-permute-start.2 = (f32[16,128]{1,0:T(8,128)S(1)}, f32[16,128]{1,0:T(8,128)S(1)}, u32[]{:S(2)}, u32[]{:S(2)}) collective-permute-start(f32[16,128]{1,0:T(8,128)S(1)} %get-tuple-element.749), channel_id=1, source_target_pairs={{0,8},{8,0},{16,24},{24,16},{1,9},{9,1},{17,25},{25,17},{2,10},{10... | collective-permute-start | bytes 24584 | tf_op jit(solution)/shard_map/while/body/eval_jaxpr/ppermute | solution.py:321
  33.2 12.4 %collective-permute-start.4 = (f32[32,128]{1,0:T(8,128)S(1)}, f32[32,128]{1,0:T(8,128)S(1)}, u32[]{:S(2)}, u32[]{:S(2)}) collective-permute-start(f32[32,128]{1,0:T(8,128)S(1)} %get-tuple-element.751), channel_id=1, source_target_pairs={{0,1},{1,0},{2,3},{3,2},{4,5},{5,4},{6,7},{7,6},{8,9},{9,8},{10,11... | collective-permute-start | bytes 49160 | tf_op jit(solution)/shard_map/while/body/eval_jaxpr/ppermute | solution.py:321
  35.2 10.4 %collective-permute-start.5 = (f32[32,128]{1,0:T(8,128)S(1)}, f32[32,128]{1,0:T(8,128)S(1)}, u32[]{:S(2)}, u32[]{:S(2)}) collective-permute-start(f32[32,128]{1,0:T(8,128)S(1)} %get-tuple-element.751), channel_id=1, source_target_pairs={{0,7},{1,2},{2,1},{3,4},{4,3},{5,6},{6,5},{7,0},{8,15},{9,10},{10,... | collective-permute-start | bytes 49160 | tf_op jit(solution)/shard_map/while/body/eval_jaxpr/ppermute | solution.py:321
  36.7 9.0 %collective-permute-start = (f32[32,128]{1,0:T(8,128)S(1)}, f32[32,128]{1,0:T(8,128)S(1)}, u32[]{:S(2)}, u32[]{:S(2)}) collective-permute-start(f32[32,128]{1,0:T(8,128)S(1)} %get-tuple-element.747), channel_id=1, source_target_pairs={{0,32},{32,0},{64,96},{96,64},{128,160},{160,128},{192,224},{224,1... | collective-permute-start | bytes 49160 | tf_op jit(solution)/shard_map/while/body/eval_jaxpr/ppermute | solution.py:321
  38.2 7.5 %collective-permute-start.1 = (f32[32,128]{1,0:T(8,128)S(1)}, f32[32,128]{1,0:T(8,128)S(1)}, u32[]{:S(2)}, u32[]{:S(2)}) collective-permute-start(f32[32,128]{1,0:T(8,128)S(1)} %get-tuple-element.748), channel_id=1, source_target_pairs={{0,224},{32,64},{64,32},{96,128},{128,96},{160,192},{192,160},{224... | collective-permute-start | bytes 49160 | tf_op jit(solution)/shard_map/while/body/eval_jaxpr/ppermute | solution.py:321
  41.0 4.6 %collective-permute-start.3 = (f32[16,128]{1,0:T(8,128)S(1)}, f32[16,128]{1,0:T(8,128)S(1)}, u32[]{:S(2)}, u32[]{:S(2)}) collective-permute-start(f32[16,128]{1,0:T(8,128)S(1)} %get-tuple-element.750), channel_id=1, source_target_pairs={{0,24},{8,16},{16,8},{24,0},{1,25},{9,17},{17,9},{25,1},{2,26},{10... | collective-permute-start | bytes 24584 | tf_op jit(solution)/shard_map/while/body/eval_jaxpr/ppermute | solution.py:321
  48.4 22.4 %all-to-all-start.1 = ((f32[256,1,128]{2,1,0:T(1,128)}), f32[256,1,128]{2,1,0:T(1,128)S(1)}, u32[]{:S(2)}, u32[]{:S(2)}) async-start(f32[256,1,128]{2,1,0:T(1,128)} %bitcast.40), calls=%async_computation.1 | async-start | bytes 262144 | tf_op jit(solution)/shard_map/while/body/eval_jaxpr/all_to_all | solution.py:326
  58.1 8.0 %collective-permute-start.8 = (f32[16,128]{1,0:T(8,128)S(1)}, f32[16,128]{1,0:T(8,128)S(1)}, u32[]{:S(2)}, u32[]{:S(2)}) collective-permute-start(f32[16,128]{1,0:T(8,128)S(1)} %get-tuple-element.687), channel_id=1, source_target_pairs={{0,8},{8,0},{16,24},{24,16},{1,9},{9,1},{17,25},{25,17},{2,10},{10... | collective-permute-start | bytes 24584 | tf_op jit(solution)/shard_map/while/body/eval_jaxpr/ppermute | solution.py:321
  58.3 12.4 %collective-permute-start.10 = (f32[32,128]{1,0:T(8,128)S(1)}, f32[32,128]{1,0:T(8,128)S(1)}, u32[]{:S(2)}, u32[]{:S(2)}) collective-permute-start(f32[32,128]{1,0:T(8,128)S(1)} %get-tuple-element.689), channel_id=1, source_target_pairs={{0,1},{1,0},{2,3},{3,2},{4,5},{5,4},{6,7},{7,6},{8,9},{9,8},{10,11... | collective-permute-start | bytes 49160 | tf_op jit(solution)/shard_map/while/body/eval_jaxpr/ppermute | solution.py:321
  60.3 10.4 %collective-permute-start.11 = (f32[32,128]{1,0:T(8,128)S(1)}, f32[32,128]{1,0:T(8,128)S(1)}, u32[]{:S(2)}, u32[]{:S(2)}) collective-permute-start(f32[32,128]{1,0:T(8,128)S(1)} %get-tuple-element.689), channel_id=1, source_target_pairs={{0,7},{1,2},{2,1},{3,4},{4,3},{5,6},{6,5},{7,0},{8,15},{9,10},{10,... | collective-permute-start | bytes 49160 | tf_op jit(solution)/shard_map/while/body/eval_jaxpr/ppermute | solution.py:321
  61.7 9.0 %collective-permute-start.6 = (f32[32,128]{1,0:T(8,128)S(1)}, f32[32,128]{1,0:T(8,128)S(1)}, u32[]{:S(2)}, u32[]{:S(2)}) collective-permute-start(f32[32,128]{1,0:T(8,128)S(1)} %get-tuple-element.685), channel_id=1, source_target_pairs={{0,32},{32,0},{64,96},{96,64},{128,160},{160,128},{192,224},{224,1... | collective-permute-start | bytes 49160 | tf_op jit(solution)/shard_map/while/body/eval_jaxpr/ppermute | solution.py:321
  63.2 7.5 %collective-permute-start.7 = (f32[32,128]{1,0:T(8,128)S(1)}, f32[32,128]{1,0:T(8,128)S(1)}, u32[]{:S(2)}, u32[]{:S(2)}) collective-permute-start(f32[32,128]{1,0:T(8,128)S(1)} %get-tuple-element.686), channel_id=1, source_target_pairs={{0,224},{32,64},{64,32},{96,128},{128,96},{160,192},{192,160},{224... | collective-permute-start | bytes 49160 | tf_op jit(solution)/shard_map/while/body/eval_jaxpr/ppermute | solution.py:321
  66.1 4.6 %collective-permute-start.9 = (f32[16,128]{1,0:T(8,128)S(1)}, f32[16,128]{1,0:T(8,128)S(1)}, u32[]{:S(2)}, u32[]{:S(2)}) collective-permute-start(f32[16,128]{1,0:T(8,128)S(1)} %get-tuple-element.688), channel_id=1, source_target_pairs={{0,24},{8,16},{16,8},{24,0},{1,25},{9,17},{17,9},{25,1},{2,26},{10... | collective-permute-start | bytes 24584 | tf_op jit(solution)/shard_map/while/body/eval_jaxpr/ppermute | solution.py:321
  73.4 22.4 %all-to-all-start = ((f32[256,1,128]{2,1,0:T(1,128)}), f32[256,1,128]{2,1,0:T(1,128)S(1)}, u32[]{:S(2)}, u32[]{:S(2)}) async-start(f32[256,1,128]{2,1,0:T(1,128)} %bitcast.38), calls=%async_computation | async-start | bytes 262144 | tf_op jit(solution)/shard_map/while/body/eval_jaxpr/all_to_all | solution.py:326
  83.1 8.0 %collective-permute-start.2 = (f32[16,128]{1,0:T(8,128)S(1)}, f32[16,128]{1,0:T(8,128)S(1)}, u32[]{:S(2)}, u32[]{:S(2)}) collective-permute-start(f32[16,128]{1,0:T(8,128)S(1)} %get-tuple-element.749), channel_id=1, source_target_pairs={{0,8},{8,0},{16,24},{24,16},{1,9},{9,1},{17,25},{25,17},{2,10},{10... | collective-permute-start | bytes 24584 | tf_op jit(solution)/shard_map/while/body/eval_jaxpr/ppermute | solution.py:321
  83.3 12.4 %collective-permute-start.4 = (f32[32,128]{1,0:T(8,128)S(1)}, f32[32,128]{1,0:T(8,128)S(1)}, u32[]{:S(2)}, u32[]{:S(2)}) collective-permute-start(f32[32,128]{1,0:T(8,128)S(1)} %get-tuple-element.751), channel_id=1, source_target_pairs={{0,1},{1,0},{2,3},{3,2},{4,5},{5,4},{6,7},{7,6},{8,9},{9,8},{10,11... | collective-permute-start | bytes 49160 | tf_op jit(solution)/shard_map/while/body/eval_jaxpr/ppermute | solution.py:321
  85.3 10.4 %collective-permute-start.5 = (f32[32,128]{1,0:T(8,128)S(1)}, f32[32,128]{1,0:T(8,128)S(1)}, u32[]{:S(2)}, u32[]{:S(2)}) collective-permute-start(f32[32,128]{1,0:T(8,128)S(1)} %get-tuple-element.751), channel_id=1, source_target_pairs={{0,7},{1,2},{2,1},{3,4},{4,3},{5,6},{6,5},{7,0},{8,15},{9,10},{10,... | collective-permute-start | bytes 49160 | tf_op jit(solution)/shard_map/while/body/eval_jaxpr/ppermute | solution.py:321
  86.8 9.0 %collective-permute-start = (f32[32,128]{1,0:T(8,128)S(1)}, f32[32,128]{1,0:T(8,128)S(1)}, u32[]{:S(2)}, u32[]{:S(2)}) collective-permute-start(f32[32,128]{1,0:T(8,128)S(1)} %get-tuple-element.747), channel_id=1, source_target_pairs={{0,32},{32,0},{64,96},{96,64},{128,160},{160,128},{192,224},{224,1... | collective-permute-start | bytes 49160 | tf_op jit(solution)/shard_map/while/body/eval_jaxpr/ppermute | solution.py:321
  88.3 7.5 %collective-permute-start.1 = (f32[32,128]{1,0:T(8,128)S(1)}, f32[32,128]{1,0:T(8,128)S(1)}, u32[]{:S(2)}, u32[]{:S(2)}) collective-permute-start(f32[32,128]{1,0:T(8,128)S(1)} %get-tuple-element.748), channel_id=1, source_target_pairs={{0,224},{32,64},{64,32},{96,128},{128,96},{160,192},{192,160},{224... | collective-permute-start | bytes 49160 | tf_op jit(solution)/shard_map/while/body/eval_jaxpr/ppermute | solution.py:321
  91.2 4.6 %collective-permute-start.3 = (f32[16,128]{1,0:T(8,128)S(1)}, f32[16,128]{1,0:T(8,128)S(1)}, u32[]{:S(2)}, u32[]{:S(2)}) collective-permute-start(f32[16,128]{1,0:T(8,128)S(1)} %get-tuple-element.750), channel_id=1, source_target_pairs={{0,24},{8,16},{16,8},{24,0},{1,25},{9,17},{17,9},{25,1},{2,26},{10... | collective-permute-start | bytes 24584 | tf_op jit(solution)/shard_map/while/body/eval_jaxpr/ppermute | solution.py:321
  98.5 22.4 %all-to-all-start.1 = ((f32[256,1,128]{2,1,0:T(1,128)}), f32[256,1,128]{2,1,0:T(1,128)S(1)}, u32[]{:S(2)}, u32[]{:S(2)}) async-start(f32[256,1,128]{2,1,0:T(1,128)} %bitcast.40), calls=%async_computation.1 | async-start | bytes 262144 | tf_op jit(solution)/shard_map/while/body/eval_jaxpr/all_to_all | solution.py:326
  108.2 8.0 %collective-permute-start.8 = (f32[16,128]{1,0:T(8,128)S(1)}, f32[16,128]{1,0:T(8,128)S(1)}, u32[]{:S(2)}, u32[]{:S(2)}) collective-permute-start(f32[16,128]{1,0:T(8,128)S(1)} %get-tuple-element.687), channel_id=1, source_target_pairs={{0,8},{8,0},{16,24},{24,16},{1,9},{9,1},{17,25},{25,17},{2,10},{10... | collective-permute-start | bytes 24584 | tf_op jit(solution)/shard_map/while/body/eval_jaxpr/ppermute | solution.py:321
  108.4 12.4 %collective-permute-start.10 = (f32[32,128]{1,0:T(8,128)S(1)}, f32[32,128]{1,0:T(8,128)S(1)}, u32[]{:S(2)}, u32[]{:S(2)}) collective-permute-start(f32[32,128]{1,0:T(8,128)S(1)} %get-tuple-element.689), channel_id=1, source_target_pairs={{0,1},{1,0},{2,3},{3,2},{4,5},{5,4},{6,7},{7,6},{8,9},{9,8},{10,11... | collective-permute-start | bytes 49160 | tf_op jit(solution)/shard_map/while/body/eval_jaxpr/ppermute | solution.py:321
  110.4 10.4 %collective-permute-start.11 = (f32[32,128]{1,0:T(8,128)S(1)}, f32[32,128]{1,0:T(8,128)S(1)}, u32[]{:S(2)}, u32[]{:S(2)}) collective-permute-start(f32[32,128]{1,0:T(8,128)S(1)} %get-tuple-element.689), channel_id=1, source_target_pairs={{0,7},{1,2},{2,1},{3,4},{4,3},{5,6},{6,5},{7,0},{8,15},{9,10},{10,... | collective-permute-start | bytes 49160 | tf_op jit(solution)/shard_map/while/body/eval_jaxpr/ppermute | solution.py:321
  111.9 9.0 %collective-permute-start.6 = (f32[32,128]{1,0:T(8,128)S(1)}, f32[32,128]{1,0:T(8,128)S(1)}, u32[]{:S(2)}, u32[]{:S(2)}) collective-permute-start(f32[32,128]{1,0:T(8,128)S(1)} %get-tuple-element.685), channel_id=1, source_target_pairs={{0,32},{32,0},{64,96},{96,64},{128,160},{160,128},{192,224},{224,1... | collective-permute-start | bytes 49160 | tf_op jit(solution)/shard_map/while/body/eval_jaxpr/ppermute | solution.py:321
  113.3 7.5 %collective-permute-start.7 = (f32[32,128]{1,0:T(8,128)S(1)}, f32[32,128]{1,0:T(8,128)S(1)}, u32[]{:S(2)}, u32[]{:S(2)}) collective-permute-start(f32[32,128]{1,0:T(8,128)S(1)} %get-tuple-element.686), channel_id=1, source_target_pairs={{0,224},{32,64},{64,32},{96,128},{128,96},{160,192},{192,160},{224... | collective-permute-start | bytes 49160 | tf_op jit(solution)/shard_map/while/body/eval_jaxpr/ppermute | solution.py:321
  116.2 4.6 %collective-permute-start.9 = (f32[16,128]{1,0:T(8,128)S(1)}, f32[16,128]{1,0:T(8,128)S(1)}, u32[]{:S(2)}, u32[]{:S(2)}) collective-permute-start(f32[16,128]{1,0:T(8,128)S(1)} %get-tuple-element.688), channel_id=1, source_target_pairs={{0,24},{8,16},{16,8},{24,0},{1,25},{9,17},{17,9},{25,1},{2,26},{10... | collective-permute-start | bytes 24584 | tf_op jit(solution)/shard_map/while/body/eval_jaxpr/ppermute | solution.py:321
  123.5 22.4 %all-to-all-start = ((f32[256,1,128]{2,1,0:T(1,128)}), f32[256,1,128]{2,1,0:T(1,128)S(1)}, u32[]{:S(2)}, u32[]{:S(2)}) async-start(f32[256,1,128]{2,1,0:T(1,128)} %bitcast.38), calls=%async_computation | async-start | bytes 262144 | tf_op jit(solution)/shard_map/while/body/eval_jaxpr/all_to_all | solution.py:326
  133.2 8.0 %collective-permute-start.2 = (f32[16,128]{1,0:T(8,128)S(1)}, f32[16,128]{1,0:T(8,128)S(1)}, u32[]{:S(2)}, u32[]{:S(2)}) collective-permute-start(f32[16,128]{1,0:T(8,128)S(1)} %get-tuple-element.749), channel_id=1, source_target_pairs={{0,8},{8,0},{16,24},{24,16},{1,9},{9,1},{17,25},{25,17},{2,10},{10... | collective-permute-start | bytes 24584 | tf_op jit(solution)/shard_map/while/body/eval_jaxpr/ppermute | solution.py:321
  133.5 12.4 %collective-permute-start.4 = (f32[32,128]{1,0:T(8,128)S(1)}, f32[32,128]{1,0:T(8,128)S(1)}, u32[]{:S(2)}, u32[]{:S(2)}) collective-permute-start(f32[32,128]{1,0:T(8,128)S(1)} %get-tuple-element.751), channel_id=1, source_target_pairs={{0,1},{1,0},{2,3},{3,2},{4,5},{5,4},{6,7},{7,6},{8,9},{9,8},{10,11... | collective-permute-start | bytes 49160 | tf_op jit(solution)/shard_map/while/body/eval_jaxpr/ppermute | solution.py:321
  135.5 10.4 %collective-permute-start.5 = (f32[32,128]{1,0:T(8,128)S(1)}, f32[32,128]{1,0:T(8,128)S(1)}, u32[]{:S(2)}, u32[]{:S(2)}) collective-permute-start(f32[32,128]{1,0:T(8,128)S(1)} %get-tuple-element.751), channel_id=1, source_target_pairs={{0,7},{1,2},{2,1},{3,4},{4,3},{5,6},{6,5},{7,0},{8,15},{9,10},{10,... | collective-permute-start | bytes 49160 | tf_op jit(solution)/shard_map/while/body/eval_jaxpr/ppermute | solution.py:321
  136.9 9.0 %collective-permute-start = (f32[32,128]{1,0:T(8,128)S(1)}, f32[32,128]{1,0:T(8,128)S(1)}, u32[]{:S(2)}, u32[]{:S(2)}) collective-permute-start(f32[32,128]{1,0:T(8,128)S(1)} %get-tuple-element.747), channel_id=1, source_target_pairs={{0,32},{32,0},{64,96},{96,64},{128,160},{160,128},{192,224},{224,1... | collective-permute-start | bytes 49160 | tf_op jit(solution)/shard_map/while/body/eval_jaxpr/ppermute | solution.py:321
  138.4 7.5 %collective-permute-start.1 = (f32[32,128]{1,0:T(8,128)S(1)}, f32[32,128]{1,0:T(8,128)S(1)}, u32[]{:S(2)}, u32[]{:S(2)}) collective-permute-start(f32[32,128]{1,0:T(8,128)S(1)} %get-tuple-element.748), channel_id=1, source_target_pairs={{0,224},{32,64},{64,32},{96,128},{128,96},{160,192},{192,160},{224... | collective-permute-start | bytes 49160 | tf_op jit(solution)/shard_map/while/body/eval_jaxpr/ppermute | solution.py:321
  141.3 4.6 %collective-permute-start.3 = (f32[16,128]{1,0:T(8,128)S(1)}, f32[16,128]{1,0:T(8,128)S(1)}, u32[]{:S(2)}, u32[]{:S(2)}) collective-permute-start(f32[16,128]{1,0:T(8,128)S(1)} %get-tuple-element.750), channel_id=1, source_target_pairs={{0,24},{8,16},{16,8},{24,0},{1,25},{9,17},{17,9},{25,1},{2,26},{10... | collective-permute-start | bytes 24584 | tf_op jit(solution)/shard_map/while/body/eval_jaxpr/ppermute | solution.py:321
  148.6 22.4 %all-to-all-start.1 = ((f32[256,1,128]{2,1,0:T(1,128)}), f32[256,1,128]{2,1,0:T(1,128)S(1)}, u32[]{:S(2)}, u32[]{:S(2)}) async-start(f32[256,1,128]{2,1,0:T(1,128)} %bitcast.40), calls=%async_computation.1 | async-start | bytes 262144 | tf_op jit(solution)/shard_map/while/body/eval_jaxpr/all_to_all | solution.py:326
  158.3 8.0 %collective-permute-start.8 = (f32[16,128]{1,0:T(8,128)S(1)}, f32[16,128]{1,0:T(8,128)S(1)}, u32[]{:S(2)}, u32[]{:S(2)}) collective-permute-start(f32[16,128]{1,0:T(8,128)S(1)} %get-tuple-element.687), channel_id=1, source_target_pairs={{0,8},{8,0},{16,24},{24,16},{1,9},{9,1},{17,25},{25,17},{2,10},{10... | collective-permute-start | bytes 24584 | tf_op jit(solution)/shard_map/while/body/eval_jaxpr/ppermute | solution.py:321
  158.5 12.4 %collective-permute-start.10 = (f32[32,128]{1,0:T(8,128)S(1)}, f32[32,128]{1,0:T(8,128)S(1)}, u32[]{:S(2)}, u32[]{:S(2)}) collective-permute-start(f32[32,128]{1,0:T(8,128)S(1)} %get-tuple-element.689), channel_id=1, source_target_pairs={{0,1},{1,0},{2,3},{3,2},{4,5},{5,4},{6,7},{7,6},{8,9},{9,8},{10,11... | collective-permute-start | bytes 49160 | tf_op jit(solution)/shard_map/while/body/eval_jaxpr/ppermute | solution.py:321
  160.5 10.4 %collective-permute-start.11 = (f32[32,128]{1,0:T(8,128)S(1)}, f32[32,128]{1,0:T(8,128)S(1)}, u32[]{:S(2)}, u32[]{:S(2)}) collective-permute-start(f32[32,128]{1,0:T(8,128)S(1)} %get-tuple-element.689), channel_id=1, source_target_pairs={{0,7},{1,2},{2,1},{3,4},{4,3},{5,6},{6,5},{7,0},{8,15},{9,10},{10,... | collective-permute-start | bytes 49160 | tf_op jit(solution)/shard_map/while/body/eval_jaxpr/ppermute | solution.py:321
  162.0 9.0 %collective-permute-start.6 = (f32[32,128]{1,0:T(8,128)S(1)}, f32[32,128]{1,0:T(8,128)S(1)}, u32[]{:S(2)}, u32[]{:S(2)}) collective-permute-start(f32[32,128]{1,0:T(8,128)S(1)} %get-tuple-element.685), channel_id=1, source_target_pairs={{0,32},{32,0},{64,96},{96,64},{128,160},{160,128},{192,224},{224,1... | collective-permute-start | bytes 49160 | tf_op jit(solution)/shard_map/while/body/eval_jaxpr/ppermute | solution.py:321
  163.4 7.5 %collective-permute-start.7 = (f32[32,128]{1,0:T(8,128)S(1)}, f32[32,128]{1,0:T(8,128)S(1)}, u32[]{:S(2)}, u32[]{:S(2)}) collective-permute-start(f32[32,128]{1,0:T(8,128)S(1)} %get-tuple-element.686), channel_id=1, source_target_pairs={{0,224},{32,64},{64,32},{96,128},{128,96},{160,192},{192,160},{224... | collective-permute-start | bytes 49160 | tf_op jit(solution)/shard_map/while/body/eval_jaxpr/ppermute | solution.py:321
  166.3 4.6 %collective-permute-start.9 = (f32[16,128]{1,0:T(8,128)S(1)}, f32[16,128]{1,0:T(8,128)S(1)}, u32[]{:S(2)}, u32[]{:S(2)}) collective-permute-start(f32[16,128]{1,0:T(8,128)S(1)} %get-tuple-element.688), channel_id=1, source_target_pairs={{0,24},{8,16},{16,8},{24,0},{1,25},{9,17},{17,9},{25,1},{2,26},{10... | collective-permute-start | bytes 24584 | tf_op jit(solution)/shard_map/while/body/eval_jaxpr/ppermute | solution.py:321
  173.7 22.6 %all-to-all-start.2 = ((f32[256,1,128]{2,1,0:T(1,128)}), f32[256,1,128]{2,1,0:T(1,128)S(1)}, u32[]{:S(2)}, u32[]{:S(2)}) async-start(f32[256,1,128]{2,1,0:T(1,128)} %bitcast.14), calls=%async_computation.2 | async-start | bytes 262144 | tf_op jit(solution)/shard_map/all_to_all | solution.py:326
  183.4 8.2 %collective-permute-start.20 = (f32[16,128]{1,0:T(8,128)S(1)}, f32[16,128]{1,0:T(8,128)S(1)}, u32[]{:S(2)}, u32[]{:S(2)}) collective-permute-start(f32[16,128]{1,0:T(8,128)S(1)} %get-tuple-element.455), channel_id=1, source_target_pairs={{0,8},{8,0},{16,24},{24,16},{1,9},{9,1},{17,25},{25,17},{2,10},{10... | collective-permute-start | bytes 24584 | tf_op jit(solution)/shard_map/ppermute | solution.py:321
  183.8 12.4 %collective-permute-start.22 = (f32[32,128]{1,0:T(8,128)S(1)}, f32[32,128]{1,0:T(8,128)S(1)}, u32[]{:S(2)}, u32[]{:S(2)}) collective-permute-start(f32[32,128]{1,0:T(8,128)S(1)} %get-tuple-element.457), channel_id=1, source_target_pairs={{0,1},{1,0},{2,3},{3,2},{4,5},{5,4},{6,7},{7,6},{8,9},{9,8},{10,11... | collective-permute-start | bytes 49160 | tf_op jit(solution)/shard_map/ppermute | solution.py:321
  185.8 10.4 %collective-permute-start.23 = (f32[32,128]{1,0:T(8,128)S(1)}, f32[32,128]{1,0:T(8,128)S(1)}, u32[]{:S(2)}, u32[]{:S(2)}) collective-permute-start(f32[32,128]{1,0:T(8,128)S(1)} %get-tuple-element.457), channel_id=1, source_target_pairs={{0,7},{1,2},{2,1},{3,4},{4,3},{5,6},{6,5},{7,0},{8,15},{9,10},{10,... | collective-permute-start | bytes 49160 | tf_op jit(solution)/shard_map/ppermute | solution.py:321
  187.2 9.0 %collective-permute-start.18 = (f32[32,128]{1,0:T(8,128)S(1)}, f32[32,128]{1,0:T(8,128)S(1)}, u32[]{:S(2)}, u32[]{:S(2)}) collective-permute-start(f32[32,128]{1,0:T(8,128)S(1)} %get-tuple-element.453), channel_id=1, source_target_pairs={{0,32},{32,0},{64,96},{96,64},{128,160},{160,128},{192,224},{224,1... | collective-permute-start | bytes 49160 | tf_op jit(solution)/shard_map/ppermute | solution.py:321
  188.7 7.5 %collective-permute-start.19 = (f32[32,128]{1,0:T(8,128)S(1)}, f32[32,128]{1,0:T(8,128)S(1)}, u32[]{:S(2)}, u32[]{:S(2)}) collective-permute-start(f32[32,128]{1,0:T(8,128)S(1)} %get-tuple-element.454), channel_id=1, source_target_pairs={{0,224},{32,64},{64,32},{96,128},{128,96},{160,192},{192,160},{224... | collective-permute-start | bytes 49160 | tf_op jit(solution)/shard_map/ppermute | solution.py:321
  191.6 4.6 %collective-permute-start.21 = (f32[16,128]{1,0:T(8,128)S(1)}, f32[16,128]{1,0:T(8,128)S(1)}, u32[]{:S(2)}, u32[]{:S(2)}) collective-permute-start(f32[16,128]{1,0:T(8,128)S(1)} %get-tuple-element.456), channel_id=1, source_target_pairs={{0,24},{8,16},{16,8},{24,0},{1,25},{9,17},{17,9},{25,1},{2,26},{10... | collective-permute-start | bytes 24584 | tf_op jit(solution)/shard_map/ppermute | solution.py:321
  222.1 18.7 %all-to-all-start.4 = ((f32[256,1,128]{2,1,0:T(1,128)}), f32[256,1,128]{2,1,0:T(1,128)S(1)}, u32[]{:S(2)}, u32[]{:S(2)}) async-start(f32[256,1,128]{2,1,0:T(1,128)} %bitcast.20), calls=%async_computation.4 | async-start | bytes 262144 | tf_op jit(solution)/shard_map/all_to_all | solution.py:326
